TPU v7x, 16 devices: a whole 2x2x2 slice. The times are simulated.
16 devices in a mesh: tp: 2 (over z), dp: 8 (over y, x, core).
Axes of the slice: x: 2, y: 2, z: 2, core: 2. Of those that a mesh axis runs over, the one named last changes fastest.
Arguments:
- h_main: bfloat16 [8, 512, 4096], P('dp')
- h_mtp: bfloat16 [8, 512, 4096], P('dp')
- labels_main: int32 [8, 512], P('dp')
- labels_mtp: int32 [8, 512], P('dp')
- weight_main: float32 [8, 512], P('dp')
- weight_mtp: float32 [8, 512], P('dp')
- gain_final: float32 [4096], replicated
- gain_mtp: float32 [4096], replicated
- w_out: bfloat16 [4096, 32256], P(None, 'tp')
Outputs:
- output 1: float32 [], replicated
- output 2: bfloat16 [8, 512, 4096], P('dp')
- output 3: bfloat16 [8, 512, 4096], P('dp')
- output 4: float32 [4096, 32256], P('dp', 'tp')
- output 5: float32 [4096], replicated
- output 6: float32 [4096], replicated
All inputs are finite; a program needn't handle non-finite values.
Results may differ from a plain program's by a relative error of at most 0.00844935.
Values sent between devices are 32-bit elements.
A program may use at most 1 GiB of HBM per device.

v0:
```python
import jax
import jax.numpy as jnp
from jax import lax
from jax.sharding import PartitionSpec as P

NORM_EPS = 1e-6
MTP_LAMBDA = 0.3


def solution(mesh):
    def local_step(h_main, h_mtp, labels_main, labels_mtp, weight_main, weight_mtp, gain_final, gain_mtp, w_out):
        batch_loc, seq_len, d_model = h_main.shape
        shard_vocab = w_out.shape[1]
        rows = batch_loc * seq_len
        weight_sums = lax.psum(jnp.stack([jnp.sum(weight_main), jnp.sum(weight_mtp)]), 'dp')
        loss_coefs = jnp.stack([1.0 / weight_sums[0], MTP_LAMBDA / weight_sums[1]])
        row_w = (jnp.stack([weight_main, weight_mtp]).reshape(2, rows) * loss_coefs[:, None]).reshape(2 * rows)
        x_rows = jnp.stack([h_main, h_mtp]).reshape(2, rows, d_model).astype(jnp.float32)
        gain_rows = jnp.stack([gain_final, gain_mtp])[:, None, :]
        inv_rms = lax.rsqrt(jnp.mean(x_rows * x_rows, axis=-1, keepdims=True) + NORM_EPS)
        normed = x_rows * inv_rms
        u_rows = (normed * gain_rows).astype(jnp.bfloat16).reshape(2 * rows, d_model)
        logits = jnp.dot(u_rows, w_out, preferred_element_type=jnp.float32)
        vocab_start = lax.axis_index('tp') * shard_vocab
        local_labels = jnp.stack([labels_main, labels_mtp]).reshape(2 * rows) - vocab_start
        is_target = jnp.arange(shard_vocab, dtype=jnp.int32)[None, :] == local_labels[:, None]
        row_max = lax.pmax(jnp.max(logits, axis=-1), 'tp')
        shifted = jnp.exp(logits - row_max[:, None])
        row_stats = lax.psum(jnp.stack([jnp.sum(shifted, axis=-1), jnp.sum(jnp.where(is_target, logits, 0.0), axis=-1)]), 'tp')
        log_norm = row_max + jnp.log(row_stats[0])
        loss_total = lax.psum(jnp.sum(row_w * (log_norm - row_stats[1])), 'dp')
        soft_probs = shifted * (1.0 / row_stats[0])[:, None]
        grad_z = (row_w[:, None] * jnp.where(is_target, soft_probs - 1.0, soft_probs)).astype(jnp.bfloat16)
        grad_w = lax.dot_general(u_rows, grad_z, (((0,), (0,)), ((), ())), preferred_element_type=jnp.float32)
        grad_w = lax.psum_scatter(grad_w, 'dp', scatter_dimension=0, tiled=True)
        grad_part = lax.dot_general(grad_z, w_out, (((1,), (1,)), ((), ())), preferred_element_type=jnp.float32).astype(jnp.bfloat16)
        grad_u = lax.psum(grad_part.astype(jnp.float32), 'tp').reshape(2, rows, d_model)
        grad_normed = grad_u * gain_rows
        grad_gain = lax.psum(jnp.sum(grad_u * normed, axis=1), 'dp')
        grad_x = inv_rms * (grad_normed - normed * jnp.mean(grad_normed * normed, axis=-1, keepdims=True))
        grad_h = grad_x.astype(jnp.bfloat16).reshape(2, batch_loc, seq_len, d_model)
        return loss_total, grad_h[0], grad_h[1], grad_w, grad_gain[0], grad_gain[1]

    row_spec = P('dp', None)
    return jax.shard_map(local_step, mesh=mesh, in_specs=(P('dp', None, None), P('dp', None, None), row_spec, row_spec, row_spec, row_spec, P(None), P(None), P(None, 'tp')), out_specs=(P(), P('dp', None, None), P('dp', None, None), P('dp', 'tp'), P(None), P(None)), check_vma=False)
```

profile of v0, /device:TPU:0, one launch (start us, length us, event | category | flops | bytes accessed | tf_op | source)
XLA Modules:
  0.0 2017.0 jit_solution(17531812724378199726)
XLA Ops:
  8.0 0.0 all-reduce.3.cloned.1.call-start
  8.0 1.3 reduce_sum.73
  9.3 1.3 reduce_sum.72
  10.6 1.4 pad_maximum_fusion.4
  12.0 15.4 psum.35
  27.4 0.6 fusion.13
  29.4 0.1 pad_maximum_fusion.5
  29.4 0.1 broadcast_bitcast_fusion
  29.5 0.6 copy.15
  30.1 4.8 fusion.6
  34.9 0.6 add_rsqrt_fusion
  35.6 0.8 pad_maximum_fusion.1
  36.3 0.6 copy-done
  36.9 7.9 fusion.3
  44.8 149.9 %fusion.14 = (f32[1024]{0:T(1024)S(1)}, f32[1024,16128]{1,0:T(8,128)}) fusion(bf16[1024,4096]{1,0:T(8,128)(2,1)} %fusion.3, bf16[4096,16128]{1,0:T(8,128)(2,1)} %param.17), kind=kOutput, calls=%fused_computation.37 | convolution fusion | flops 135307984896 | bytes 206573568 | tf_op jit(solution)/shard_map/dot_general | solution.py:23
  194.7 4.9 pmax.7
  199.7 25.2 %fusion.2 = (f32[1024]{0:T(1024)S(1)}, f32[1024]{0:T(1024)S(1)}) fusion(f32[1024,16128]{1,0:T(8,128)} %get-tuple-element.26, f32[1024]{0:T(1024)S(1)} %pmax.7, s32[1024]{0:T(1024)S(1)} %bitcast.69), kind=kLoop, calls=%fused_computation.6 | loop fusion | flops 82573312 | bytes 66076672 | tf_op jit(solution)/shard_map/reduce_sum | solution.py:29
  224.8 5.0 psum.36
  229.9 0.6 multiply_reduce_fusion.1
  230.5 33.0 %fusion.25 = bf16[1024,16128]{1,0:T(8,128)(2,1)} fusion(f32[1024,16128]{1,0:T(8,128)} %get-tuple-element.26, f32[1024]{0:T(1024)S(1)} %bitcast.72, f32[1024]{0:T(1024)S(1)} %get-tuple-element.11, s32[1024]{0:T(1024)S(1)} %bitcast.70, f32[1024]{0:T(1024)S(1)} %pmax.7), kind=kLoop, calls=%fused_computation.2.clone.1.clone.1 | loop fusion | flops 115605504 | bytes 99106816 | tf_op jit(solution)/shard_map/dot_general | solution.py:36
  263.6 148.4 %convert_convert_fusion = f32[1024,4096]{1,0:T(8,128)} fusion(bf16[4096,16128]{1,0:T(8,128)(2,1)} %param.17, bf16[1024,16128]{1,0:T(8,128)(2,1)} %fusion.25), kind=kOutput, calls=%fused_computation.19 | convolution fusion | flops 135299858432 | bytes 181927936 | tf_op jit(solution)/shard_map/dot_general | solution.py:36
  412.0 0.3 reduce-scatter.2.cloned.1.call-start
  412.3 0.4 copy-done.3
  412.6 0.0 copy-done.7
  412.6 167.7 %fusion.8 = f32[4096,16128]{1,0:T(8,128)} fusion(bf16[1024,4096]{1,0:T(8,128)(2,1)} %fusion.3, f32[1024,16128]{1,0:T(8,128)} %get-tuple-element.26, f32[1024]{0:T(1024)S(1)} %bitcast.73, f32[1024]{0:T(1024)S(1)} %copy-done.12, s32[1024]{0:T(1024)S(1)} %bitcast.71, f32[1024]{0:T(1024)S(1)} %copy-done.3), kind=kOutput, calls=%fused_computation.33 | convolution fusion | flops 135407075328 | bytes 338706432 | tf_op jit(solution)/shard_map/dot_general | solution.py:34
  580.4 204.9 %all-reduce.3.cloned.1.call-done = f32[1024,4096]{1,0:T(8,128)} async-done(((f32[1024,4096]{1,0:T(8,128)}), f32[1024,4096]{1,0:T(8,128)}) %all-reduce.3.cloned.1.call-update) | async-done | bytes 16777232 | tf_op jit(solution)/shard_map/psum | solution.py:37
  785.3 9.3 fusion.5
  794.7 13.4 multiply_convert_fusion
  808.1 25.2 %all-reduce = (f32[]{:T(128)}, f32[2,4096]{1,0:T(2,128)S(1)}) all-reduce(f32[]{:T(128)} %get-tuple-element.10, f32[2,4096]{1,0:T(2,128)S(1)} %get-tuple-element.13), channel_id=1, replica_groups=mesh['tp'=2,'dp'=8] {'dp'}, use_global_device_ids=true, to_apply=%region_10.11 | all-reduce | flops 8193 | bytes 65544 | tf_op jit(solution)/shard_map/psum | solution.py:31
  833.3 0.6 fusion.12
  834.0 6.1 fusion.11
  840.0 1169.5 %reduce-scatter.2.cloned.1.call-done = f32[512,16128]{1,0:T(8,128)} async-done(((f32[4096,16128]{1,0:T(8,128)}), f32[512,16128]{1,0:T(8,128)}) %reduce-scatter.2.cloned.1.call-update) | async-done | bytes 33030160 | tf_op jit(solution)/shard_map/reduce_scatter | solution.py:35
  (42 shorter events, 0.2 us)
Async XLA Ops:
  8.0 777.3 %all-reduce.3.cloned.1.call-start = ((), (), s32[]{:S(2)}) async-start(), calls=%async_computation.1 | async-start | bytes 33554432 | tf_op jit(solution)/shard_map/psum | solution.py:37
  35.5 0.8 copy-start.4
  36.3 0.6 copy-start
  44.8 154.8 %copy-start.16 = (s32[1,512]{1,0:T(1,128)S(1)}, s32[1,512]{1,0:T(1,128)}, u32[]{:S(2)}) copy-start(s32[1,512]{1,0:T(1,128)} %param.12) | copy-start | bytes 6148
  44.8 154.8 %copy-start.17 = (s32[1,512]{1,0:T(1,128)S(1)}, s32[1,512]{1,0:T(1,128)}, u32[]{:S(2)}) copy-start(s32[1,512]{1,0:T(1,128)} %param.11) | copy-start | bytes 6148
  199.6 30.9 %copy-start.2 = (f32[1024]{0:T(1024)}, f32[1024]{0:T(1024)S(1)}, u32[]{:S(2)}) copy-start(f32[1024]{0:T(1024)S(1)} %pmax.7) | copy-start | bytes 12292
  199.6 30.9 %copy-start.6 = (s32[2,1,512]{2,1,0:T(1,128)}, s32[2,1,512]{2,1,0:T(1,128)S(1)}, u32[]{:S(2)}) copy-start(s32[2,1,512]{2,1,0:T(1,128)S(1)} %add_subtract_fusion) | copy-start | bytes 12292
  199.6 30.3 %copy-start.14 = (f32[1,512]{1,0:T(1,128)S(1)}, f32[1,512]{1,0:T(1,128)}, u32[]{:S(2)}) copy-start(f32[1,512]{1,0:T(1,128)} %param.14) | copy-start | bytes 6148
  199.6 30.3 %copy-start.15 = (f32[1,512]{1,0:T(1,128)S(1)}, f32[1,512]{1,0:T(1,128)}, u32[]{:S(2)}) copy-start(f32[1,512]{1,0:T(1,128)} %param.13) | copy-start | bytes 6148
  199.6 30.3 %copy-start.13 = (f32[1,4,2,128]{3,1,2,0:T(4,128)S(1)}, f32[1,4,2,128]{3,1,2,0:T(4,128)}, u32[]{:S(2)}) copy-start(f32[1,4,2,128]{3,1,2,0:T(4,128)} %copy.15) | copy-start | bytes 12292
  229.9 33.7 %copy-start.9 = (f32[1,1024]{1,0:T(1,128)}, f32[1,1024]{1,0:T(1,128)S(1)}, u32[]{:S(2)}) copy-start(f32[1,1024]{1,0:T(1,128)S(1)} %get-tuple-element.18) | copy-start | bytes 12292
  230.5 33.0 %copy-start.11 = (f32[1024]{0:T(1024)}, f32[1024]{0:T(1024)S(1)}, u32[]{:S(2)}) copy-start(f32[1024]{0:T(1024)S(1)} %get-tuple-element.11) | copy-start | bytes 12292
  411.9 0.7 copy-start.3
  411.9 0.7 copy-start.7
  411.9 0.7 copy-start.10
  412.0 0.7 copy-start.12
  412.0 1597.5 %reduce-scatter.2.cloned.1.call-start = ((), (), s32[]{:S(2)}) async-start(), calls=%async_computation.2 | async-start | bytes 297271296 | tf_op jit(solution)/shard_map/reduce_scatter | solution.py:35
  580.4 204.9 %copy-start.1 = (f32[2,4096]{1,0:T(2,128)S(1)}, f32[2,4096]{1,0:T(2,128)}, u32[]{:S(2)}) copy-start(f32[2,4096]{1,0:T(2,128)} %copy-done) | copy-start | bytes 98308
  580.4 204.9 %copy-start.5 = (f32[1,4,2,128]{3,1,2,0:T(4,128)S(1)}, f32[1,4,2,128]{3,1,2,0:T(4,128)}, u32[]{:S(2)}) copy-start(f32[1,4,2,128]{3,1,2,0:T(4,128)} %copy-done.4) | copy-start | bytes 12292
  580.4 214.3 %copy-start.8 = (f32[2,512]{1,0:T(2,128)S(1)}, f32[2,512]{1,0:T(2,128)}, u32[]{:S(2)}) copy-start(f32[2,512]{1,0:T(2,128)} %get-tuple-element.21) | copy-start | bytes 12292
Sparse Core Ops, SparseCore 0:
  412.1 373.1 all-reduce.2
Sparse Core Ops, SparseCore 1:
  580.5 1428.9 reduce-scatter.1
where the time goes:
time: 2020 us
  waiting for transfers between devices  1370 us (68%)
  matrix products  466 us (23%)
  other arithmetic  99.7 us (5%)
  blocking collectives  50.5 us (2%)
    reduce_scatter x1, waiting for transfers between devices, local_step(): grad_w = lax.psum_scatter(grad_w, 'dp', scatter_dimension=0, tiled=True)  1170 us
    psum x1, waiting for transfers between devices, local_step(): lax.psum(grad_part.astype(jnp.float32), 'tp').reshape(2, rows, d_model)  205 us
    dot_general x1, matrix products, local_step(): lax.dot_general(u_rows, grad_z, (((0,), (0,)), ((), ())), preferred_eleme...  168 us
    dot_general x1, matrix products, local_step(): logits = jnp.dot(u_rows, w_out, preferred_element_type=jnp.float32)  150 us
    dot_general x1, matrix products, local_step(): lax.dot_general(grad_z, w_out, (((1,), (1,)), ((), ())), preferred_elemen...  148 us
  transfers between devices with their start and end apart: 2, of which 2 were waited for; matrix products, arithmetic and copies ran while one was open for 10% of the time, Pallas kernels for 0%

commit v1 on v0

v1 whole, which is shorter than its diff:
```python
import jax
import jax.numpy as jnp
from jax import lax
from jax.sharding import PartitionSpec as P


NORM_EPS = 1e-6
MTP_LAMBDA = 0.3
CHUNKS = 4


def solution(mesh):
    n_dp = mesh.shape['dp']
    n_tp = mesh.shape['tp']

    def layer_step(h_main, h_mtp, labels_main, labels_mtp, weight_main, weight_mtp, gain_final, gain_mtp, w_out):
        batch_loc, seq_len, d_model = h_main.shape
        shard_vocab = w_out.shape[1]
        rows = batch_loc * seq_len
        half = rows // n_tp
        dp_rank = lax.axis_index('dp')
        tp_rank = lax.axis_index('tp')
        gains = (gain_final[None, :], gain_mtp[None, :])

        normed, gathered = [], []
        for h in (h_main, h_mtp):
            x = h.reshape(rows, d_model).astype(jnp.float32)
            inv = lax.rsqrt(jnp.mean(x * x, axis=-1, keepdims=True) + NORM_EPS)
            n = x * inv
            normed.append(n)
            gathered.append(lax.all_gather(lax.dynamic_slice_in_dim(n, tp_rank * half, half, 0), ('tp', 'dp'), axis=0, tiled=True))

        vocab_start = tp_rank * shard_vocab
        column = jnp.arange(shard_vocab, dtype=jnp.int32)[None, :]
        u_own = [(n * g).astype(jnp.bfloat16) for n, g in zip(normed, gains)]
        labels_own = [l.reshape(rows) for l in (labels_main, labels_mtp)]
        weights_own = [w.reshape(rows) for w in (weight_main, weight_mtp)]
        u_rows = jnp.concatenate(u_own, axis=0)
        local_labels = jnp.concatenate(labels_own) - vocab_start
        logits = jnp.dot(u_rows, w_out, preferred_element_type=jnp.float32)
        row_max = jnp.max(logits, axis=-1)
        is_target = column == local_labels[:, None]
        row_sum = jnp.sum(jnp.exp(logits - row_max[:, None]), axis=-1)
        row_target = jnp.sum(jnp.where(is_target, logits, 0.0), axis=-1)

        stats = jnp.stack([row_max, row_sum, row_target, jnp.concatenate(labels_own).astype(jnp.float32), jnp.concatenate(weights_own)])
        stats = lax.all_gather(stats, ('tp', 'dp'), axis=0, tiled=False).reshape(n_tp, n_dp, 5, 2, rows)
        all_max = jnp.max(stats[:, :, 0], axis=0)
        all_sum = jnp.sum(stats[:, :, 1] * jnp.exp(stats[:, :, 0] - all_max[None]), axis=0)
        all_lse = all_max + jnp.log(all_sum)
        all_target = jnp.sum(stats[:, :, 2], axis=0)
        all_labels = stats[0, :, 3].astype(jnp.int32)
        all_weights = stats[0, :, 4]
        coefs = jnp.array([1.0, MTP_LAMBDA], jnp.float32) / jnp.sum(all_weights, axis=(0, 2))
        all_row_w = all_weights * coefs[None, :, None]
        loss_total = jnp.sum(all_row_w * (all_lse - all_target))

        own_lse = lax.dynamic_index_in_dim(all_lse, dp_rank, 0, keepdims=False).reshape(2 * rows)
        own_row_w = lax.dynamic_index_in_dim(all_row_w, dp_rank, 0, keepdims=False).reshape(2 * rows)
        probs = jnp.exp(logits - own_lse[:, None])
        grad_z = (own_row_w[:, None] * jnp.where(is_target, probs - 1.0, probs)).astype(jnp.bfloat16)
        grad_u = []
        for which in range(2):
            part = lax.dot_general(grad_z[which * rows:(which + 1) * rows], w_out, (((1,), (1,)), ((), ())), preferred_element_type=jnp.float32).astype(jnp.bfloat16).astype(jnp.float32)
            grad_u.append((part, lax.ppermute(part, 'tp', [(i, n_tp - 1 - i) for i in range(n_tp)])))

        width = -(-shard_vocab // (n_dp * 256)) * 256
        col_unit = jnp.minimum(dp_rank * (width // 256), (shard_vocab - width) // 256)
        w_slice = lax.dynamic_slice_in_dim(w_out, col_unit * 256, width, 1)
        slice_start = vocab_start + col_unit * 256

        def token_order(a):
            return a.reshape(n_dp, n_tp, half).transpose(1, 0, 2).reshape(n_dp * rows)

        def slice_grad(which, u_all, cols, start):
            z = jnp.dot(u_all, cols, preferred_element_type=jnp.float32)
            hit = (jnp.arange(cols.shape[1], dtype=jnp.int32)[None, :] + start) == token_order(all_labels[:, which])[:, None]
            p = jnp.exp(z - token_order(all_lse[:, which])[:, None])
            e = (token_order(all_row_w[:, which])[:, None] * jnp.where(hit, p - 1.0, p)).astype(jnp.bfloat16)
            return lax.dot_general(u_all, e, (((0,), (0,)), ((), ())), preferred_element_type=jnp.float32)

        u_all = [(n * g).astype(jnp.bfloat16) for n, g in zip(gathered, gains)]
        grad_main = slice_grad(0, u_all[0], w_slice, slice_start)
        d_loc = d_model // n_dp
        grad_w = jnp.zeros((d_loc, shard_vocab), jnp.float32)
        cw = width // CHUNKS
        for q in range(CHUNKS):
            cols = w_slice[:, q * cw:(q + 1) * cw]
            part = grad_main[:, q * cw:(q + 1) * cw] + slice_grad(1, u_all[1], cols, slice_start + q * cw)
            sends = lax.optimization_barrier([lax.dynamic_slice(part, ((dp_rank ^ k) * d_loc, 0), (d_loc, cw)) for k in range(n_dp)])
            for k, block in enumerate(sends):
                if k:
                    block = lax.ppermute(block, 'dp', [(i, i ^ k) for i in range(n_dp)])
                peer_unit = jnp.minimum((dp_rank ^ k) * (width // 256), (shard_vocab - width) // 256)
                grad_w = lax.dynamic_update_slice(grad_w, block, (0, (peer_unit + q * cw // 256) * 256))

        grads_h, gain_parts = [], []
        for which, h in enumerate((h_main, h_mtp)):
            h, part, other = lax.optimization_barrier((h, *grad_u[which]))
            x = h.reshape(rows, d_model).astype(jnp.float32)
            inv = lax.rsqrt(jnp.mean(x * x, axis=-1, keepdims=True) + NORM_EPS)
            n = x * inv
            du = part + other
            grad_normed = du * gains[which]
            gain_parts.append(jnp.sum(du * n, axis=0))
            grad_x = inv * (grad_normed - n * jnp.mean(grad_normed * n, axis=-1, keepdims=True))
            grads_h.append(grad_x.astype(jnp.bfloat16).reshape(batch_loc, seq_len, d_model))
        grad_gain = lax.psum(jnp.stack(gain_parts), 'dp')
        return loss_total, grads_h[0], grads_h[1], grad_w, grad_gain[0], grad_gain[1]


    row_spec = P('dp', None)
    return jax.shard_map(layer_step, mesh=mesh, in_specs=(P('dp', None, None), P('dp', None, None), row_spec, row_spec, row_spec, row_spec, P(None), P(None), P(None, 'tp')), out_specs=(P(), P('dp', None, None), P('dp', None, None), P('dp', 'tp'), P(None), P(None)), check_vma=False)
```

time: 2020 us -> 1680 us (0.83)
  waiting for transfers between devices: 1370 us -> 666 us
  matrix products: 466 us -> 705 us
  local copies, waits for them, and re-layouts: 9 us -> 64.9 us
  other arithmetic: 99.7 us -> 151 us
  starting transfers between devices: 0.3 us -> 25.2 us
    reduce_scatter x1 -> x0, waiting for transfers between devices: 1170 us -> none  [local_step(): grad_w = lax.psum_scatter(grad_w, 'dp', scatter_dimension=0, tiled=True)]
    ppermute x0 -> x30, waiting for transfers between devices: none -> 666 us  [the longest x2 430 us: layer_step(): lax.ppermute(part, 'tp', [(i, n_tp - 1 - i) for i in range(n_tp)])]
    dot_general x3 -> x13, matrix products: 466 us -> 705 us  [the longest x5 196 us: slice_grad(): lax.dot_general(u_all, e, (((0,), (0,)), ((), ())), preferred_element_typ...]
    psum x1 -> x0, waiting for transfers between devices: 205 us -> none  [local_step(): lax.psum(grad_part.astype(jnp.float32), 'tp').reshape(2, rows, d_model)]
    convert_element_type x2 -> x4, other arithmetic: 21.3 us -> 67.6 us  [the longest x1 33.5 us: layer_step(): (own_row_w[:, None] * jnp.where(is_target, probs - 1.0, probs)).astype(jn...]
    dot_general x1 -> x0, other arithmetic: 33 us -> none  [local_step(): lax.dot_general(grad_z, w_out, (((1,), (1,)), ((), ())), preferred_elemen...]
    ppermute x0 -> x30, starting transfers between devices: none -> 25.1 us  [the longest x28 22 us: layer_step(): block = lax.ppermute(block, 'dp', [(i, i ^ k) for i in range(n_dp)])]
    dynamic_update_slice x0 -> x32, local copies, waits for them, and re-layouts: none -> 24.4 us  [layer_step(): lax.dynamic_update_slice(grad_w, block, (0, (peer_unit + q * cw // 256) *...]
  transfers between devices with their start and end apart: 2 -> 32, of which waited for: 2 -> 16; matrix products, arithmetic and copies ran while one was open for 10% -> 41% of each run, Pallas kernels for 0% -> 0%
where the time goes in v1:
time: 1680 us; the launch traced here: 1670 us
  matrix products  705 us (42%)
  waiting for transfers between devices  666 us (40%)
  other arithmetic  151 us (9%)
  local copies, waits for them, and re-layouts  64.9 us (4%)
  blocking collectives  41.5 us (2%)
  starting transfers between devices  25.2 us (2%)
    ppermute x2, waiting for transfers between devices, layer_step(): lax.ppermute(part, 'tp', [(i, n_tp - 1 - i) for i in range(n_tp)])  430 us
    ppermute x28, waiting for transfers between devices, layer_step(): block = lax.ppermute(block, 'dp', [(i, i ^ k) for i in range(n_dp)])  237 us
    dot_general x5, matrix products, slice_grad(): lax.dot_general(u_all, e, (((0,), (0,)), ((), ())), preferred_element_typ...  196 us
    dot_general x5, matrix products, slice_grad(): z = jnp.dot(u_all, cols, preferred_element_type=jnp.float32)  190 us
    dot_general x2, matrix products, layer_step(): lax.dot_general(grad_z[which * rows:(which + 1) * rows], w_out, (((1,), (...  165 us
    dot_general x1, matrix products, layer_step(): logits = jnp.dot(u_rows, w_out, preferred_element_type=jnp.float32)  153 us
  transfers between devices with their start and end apart: 32, of which 16 were waited for; matrix products, arithmetic and copies ran while one was open for 41% of the time, Pallas kernels for 0%

profile of v1, /device:TPU:0, one launch (start us, length us, event | category | flops | bytes accessed | tf_op | source)
XLA Modules:
  0.0 1669.4 jit_solution(13971461484588280364)
XLA Ops:
  31.2 153.3 %fusion.75 = (f32[1024]{0:T(1024)S(1)}, f32[1024,16128]{1,0:T(8,128)}) fusion(bf16[4096,16128]{1,0:T(8,128)(2,1)} %param.18, bf16[512,4096]{1,0:T(8,128)(2,1)} %get-tuple-element.132, bf16[512,4096]{1,0:T(8,128)(2,1)} %get-tuple-element.139), kind=kOutput, calls=%fused_computation.190 | convolution fusion | flops 135324762112 | bytes 206573568 | tf_op jit(solution)/shard_map/dot_general | solution.py:40
  184.6 24.7 %select_reduce_fusion = (f32[1024]{0:T(1024)S(1)}, f32[1024]{0:T(1024)S(1)}) fusion(f32[1024,16128]{1,0:T(8,128)} %get-tuple-element.138, s32[1024]{0:T(1024)S(1)} %copy-done.16, f32[1024]{0:T(1024)S(1)} %get-tuple-element.137), kind=kLoop, calls=%fused_computation.5 | loop fusion | flops 82573312 | bytes 66076672 | tf_op jit(solution)/shard_map/reduce_sum | solution.py:44
  209.3 17.3 %all-gather.1 = f32[16,5,1024]{2,1,0:T(8,128)S(1)} all-gather(f32[1,5,1024]{2,1,0:T(8,128)S(1)} %bitcast.134), channel_id=2, replica_groups=mesh['tp'=2,'dp'=8] {'tp','dp'}, dimensions={0}, use_global_device_ids=true | all-gather | bytes 348160 | tf_op jit(solution)/shard_map/all_gather | solution.py:47
  228.5 33.5 %fusion.1 = bf16[1024,16128]{1,0:T(8,128)(2,1)} fusion(f32[1024,16128]{1,0:T(8,128)} %get-tuple-element.138, f32[1024]{0:T(1024)S(1)} %bitcast.143, f32[1024]{0:T(1024)S(1)} %bitcast.144, s32[1024]{0:T(1024)S(1)} %copy-done.16), kind=kLoop, calls=%fused_computation.4 | loop fusion | flops 99090432 | bytes 99102720 | tf_op jit(solution)/shard_map/convert_element_type | solution.py:61
  262.0 82.3 %fusion.45 = f32[512,4096]{1,0:T(8,128)} fusion(bf16[4096,16128]{1,0:T(8,128)(2,1)} %param.18, bf16[1024,16128]{1,0:T(8,128)(2,1)} %fusion.1), kind=kOutput, calls=%fused_computation.68 | convolution fusion | flops 67649929216 | bytes 157024256 | tf_op jit(solution)/shard_map/dot_general | solution.py:64
  347.5 83.1 %fusion.51 = f32[512,4096]{1,0:T(8,128)} fusion(bf16[4096,16128]{1,0:T(8,128)(2,1)} %param.18, bf16[1024,16128]{1,0:T(8,128)(2,1)} %fusion.1), kind=kOutput, calls=%fused_computation.70 | convolution fusion | flops 67649929216 | bytes 157024256 | tf_op jit(solution)/shard_map/dot_general | solution.py:64
  433.6 249.9 %collective-permute-done = f32[512,4096]{1,0:T(8,128)} collective-permute-done((f32[512,4096]{1,0:T(8,128)}, f32[512,4096]{1,0:T(8,128)}, u32[]{:S(2)}, u32[]{:S(2)}) %collective-permute-start) | collective-permute-done | bytes 8388640 | tf_op jit(solution)/shard_map/ppermute | solution.py:65
  683.5 179.7 %collective-permute-done.1 = f32[512,4096]{1,0:T(8,128)} collective-permute-done((f32[512,4096]{1,0:T(8,128)}, f32[512,4096]{1,0:T(8,128)}, u32[]{:S(2)}, u32[]{:S(2)}) %collective-permute-start.1) | collective-permute-done | bytes 8388640 | tf_op jit(solution)/shard_map/ppermute | solution.py:65
  883.8 24.2 %psum.7 = f32[2,4096]{1,0:T(2,128)S(1)} all-reduce(f32[2,4096]{1,0:T(2,128)S(1)} %pad_maximum_fusion), channel_id=1, replica_groups=mesh['tp'=2,'dp'=8] {'dp'}, use_global_device_ids=true, to_apply=%region_16.17 | all-reduce | flops 8192 | bytes 65536 | tf_op jit(solution)/shard_map/psum | solution.py:108
  928.3 32.7 %multiply_convert_fusion = bf16[4096,4096]{1,0:T(8,128)(2,1)} fusion(f32[4096,4096]{1,0:T(8,128)} %all-gather.7.cloned.1.call-done, f32[4096]{0:T(1024)S(1)} %copy-done.10), kind=kLoop, calls=%fused_computation.1 | loop fusion | flops 33554432 | bytes 100679680 | tf_op jit(solution)/shard_map/convert_element_type | solution.py:82
  961.0 26.2 %fusion.31 = bf16[4096,512]{1,0:T(8,128)(2,1)} fusion(bf16[4096,4096]{1,0:T(8,128)(2,1)} %multiply_convert_fusion, bf16[4096,16128]{1,0:T(8,128)(2,1)} %param.18, s32[]{:T(128)S(6)} %select_n.183, f32[4096]{0:T(1024)S(1)} %bitcast.148, s32[512]{0:T(512)S(1)} %iota_add_fusion.4, f32[4096]{0:T(1024)S(1)} %bitcast.152, s32[4096]{0:T(1024)S(1)} %bitcast.156), kind=kOutput, calls=%fused_computation.50 | convolution fusion | flops 17192452096 | bytes 41994244 | tf_op jit(solution)/shard_map/dot_general | solution.py:76
  987.2 84.9 %fusion.3 = bf16[4096,2048]{1,0:T(8,128)(2,1)} fusion(f32[4096]{0:T(1024)S(1)} %bitcast.160, bf16[4096,16128]{1,0:T(8,128)(2,1)} %param.18, s32[]{:T(128)S(6)} %select_n.183, s32[2048]{0:T(1024)S(1)} %iota_add_fusion, f32[4096]{0:T(1024)S(1)} %bitcast.161, s32[4096]{0:T(1024)S(1)} %bitcast.162, f32[4096,4096]{1,0:T(8,128)} %all-gather.5.cloned.1.call-done, ...), kind=kOutput, calls=%fused_computation.10 | convolution fusion | flops 68803362816 | bytes 100737024 | tf_op jit(solution)/shard_map/dot_general | solution.py:76
  1072.1 82.4 %fusion.9 = f32[4096,2048]{1,0:T(8,128)} fusion(bf16[4096,2048]{1,0:T(8,128)(2,1)} %fusion.3, f32[4096,4096]{1,0:T(8,128)} %all-gather.5.cloned.1.call-done, f32[4096]{0:T(1024)S(1)} %copy-done.15), kind=kOutput, calls=%fused_computation.16 | convolution fusion | flops 68753031168 | bytes 117456896 | tf_op jit(solution)/shard_map/dot_general | solution.py:80
  1154.5 28.3 %slice_add_fusion.3 = f32[4096,512]{1,0:T(8,128)} fusion(f32[4096,2048]{1,0:T(8,128)} %fusion.9, bf16[4096,4096]{1,0:T(8,128)(2,1)} %multiply_convert_fusion, bf16[4096,512]{1,0:T(8,128)(2,1)} %fusion.31), kind=kOutput, calls=%fused_computation.60 | convolution fusion | flops 17181966336 | bytes 54525952 | tf_op jit(solution)/shard_map/dot_general | solution.py:80
  1193.3 26.4 %fusion.33 = bf16[4096,512]{1,0:T(8,128)(2,1)} fusion(bf16[4096,4096]{1,0:T(8,128)(2,1)} %multiply_convert_fusion, bf16[4096,16128]{1,0:T(8,128)(2,1)} %param.18, s32[]{:T(128)S(6)} %add.453, s32[512]{0:T(512)S(1)} %copy-done.29, f32[4096]{0:T(1024)S(1)} %bitcast.149, f32[4096]{0:T(1024)S(1)} %bitcast.153, s32[4096]{0:T(1024)S(1)} %bitcast.157), kind=kOutput, calls=%fused_computation.52 | convolution fusion | flops 17192452096 | bytes 41994244 | tf_op jit(solution)/shard_map/dot_general | solution.py:76
  1219.7 28.5 %slice_add_fusion.2 = f32[4096,512]{1,0:T(8,128)} fusion(f32[4096,2048]{1,0:T(8,128)} %fusion.9, bf16[4096,4096]{1,0:T(8,128)(2,1)} %multiply_convert_fusion, bf16[4096,512]{1,0:T(8,128)(2,1)} %fusion.33), kind=kOutput, calls=%fused_computation.59 | convolution fusion | flops 17181966336 | bytes 54525952 | tf_op jit(solution)/shard_map/dot_general | solution.py:80
  1248.2 26.3 %fusion.35 = bf16[4096,512]{1,0:T(8,128)(2,1)} fusion(bf16[4096,4096]{1,0:T(8,128)(2,1)} %multiply_convert_fusion, bf16[4096,16128]{1,0:T(8,128)(2,1)} %param.18, s32[]{:T(128)S(6)} %add.454, s32[512]{0:T(512)S(1)} %copy-done.28, f32[4096]{0:T(1024)S(1)} %bitcast.150, f32[4096]{0:T(1024)S(1)} %bitcast.154, s32[4096]{0:T(1024)S(1)} %bitcast.158), kind=kOutput, calls=%fused_computation.54 | convolution fusion | flops 17192452096 | bytes 41994244 | tf_op jit(solution)/shard_map/dot_general | solution.py:76
  1274.5 28.3 %slice_add_fusion.1 = f32[4096,512]{1,0:T(8,128)} fusion(f32[4096,2048]{1,0:T(8,128)} %fusion.9, bf16[4096,4096]{1,0:T(8,128)(2,1)} %multiply_convert_fusion, bf16[4096,512]{1,0:T(8,128)(2,1)} %fusion.35), kind=kOutput, calls=%fused_computation.58 | convolution fusion | flops 17181966336 | bytes 54525952 | tf_op jit(solution)/shard_map/dot_general | solution.py:80
  1302.8 26.5 %fusion.37 = bf16[4096,512]{1,0:T(8,128)(2,1)} fusion(bf16[4096,4096]{1,0:T(8,128)(2,1)} %multiply_convert_fusion, bf16[4096,16128]{1,0:T(8,128)(2,1)} %param.18, s32[]{:T(128)S(6)} %add.455, s32[512]{0:T(512)S(1)} %copy-done.27, f32[4096]{0:T(1024)S(1)} %bitcast.151, f32[4096]{0:T(1024)S(1)} %bitcast.155, s32[4096]{0:T(1024)S(1)} %bitcast.159), kind=kOutput, calls=%fused_computation.56 | convolution fusion | flops 17192452096 | bytes 41994244 | tf_op jit(solution)/shard_map/dot_general | solution.py:76
  1335.5 28.3 %slice_add_fusion = f32[4096,512]{1,0:T(8,128)} fusion(f32[4096,2048]{1,0:T(8,128)} %fusion.9, bf16[4096,4096]{1,0:T(8,128)(2,1)} %multiply_convert_fusion, bf16[4096,512]{1,0:T(8,128)(2,1)} %fusion.37), kind=kOutput, calls=%fused_computation.57 | convolution fusion | flops 17181966336 | bytes 54525952 | tf_op jit(solution)/shard_map/dot_general | solution.py:80
  1389.5 13.9 collective-permute-done.10
  1404.9 20.0 %collective-permute-done.11 = f32[512,512]{1,0:T(8,128)} collective-permute-done((f32[512,512]{1,0:T(8,128)}, f32[512,512]{1,0:T(8,128)}, u32[]{:S(2)}, u32[]{:S(2)}) %collective-permute-start.11) | collective-permute-done | bytes 1048608 | tf_op jit(solution)/shard_map/ppermute | solution.py:93
  1431.4 18.0 %collective-permute-done.14 = f32[512,512]{1,0:T(8,128)} collective-permute-done((f32[512,512]{1,0:T(8,128)}, f32[512,512]{1,0:T(8,128)}, u32[]{:S(2)}, u32[]{:S(2)}) %collective-permute-start.14) | collective-permute-done | bytes 1048608 | tf_op jit(solution)/shard_map/ppermute | solution.py:93
  1453.9 16.8 %collective-permute-done.15 = f32[512,512]{1,0:T(8,128)S(1)} collective-permute-done((f32[512,512]{1,0:T(8,128)}, f32[512,512]{1,0:T(8,128)S(1)}, u32[]{:S(2)}, u32[]{:S(2)}) %collective-permute-start.15) | collective-permute-done | bytes 1048608 | tf_op jit(solution)/shard_map/ppermute | solution.py:93
  1475.6 17.7 %collective-permute-done.17 = f32[512,512]{1,0:T(8,128)S(1)} collective-permute-done((f32[512,512]{1,0:T(8,128)}, f32[512,512]{1,0:T(8,128)S(1)}, u32[]{:S(2)}, u32[]{:S(2)}) %collective-permute-start.17) | collective-permute-done | bytes 1048608 | tf_op jit(solution)/shard_map/ppermute | solution.py:93
  1494.8 19.9 %collective-permute-done.18 = f32[512,512]{1,0:T(8,128)S(1)} collective-permute-done((f32[512,512]{1,0:T(8,128)}, f32[512,512]{1,0:T(8,128)S(1)}, u32[]{:S(2)}, u32[]{:S(2)}) %collective-permute-start.18) | collective-permute-done | bytes 1048608 | tf_op jit(solution)/shard_map/ppermute | solution.py:93
  1519.0 20.3 %collective-permute-done.21 = f32[512,512]{1,0:T(8,128)} collective-permute-done((f32[512,512]{1,0:T(8,128)S(1)}, f32[512,512]{1,0:T(8,128)}, u32[]{:S(2)}, u32[]{:S(2)}) %collective-permute-start.21) | collective-permute-done | bytes 1048608 | tf_op jit(solution)/shard_map/ppermute | solution.py:93
  1541.1 19.6 %collective-permute-done.22 = f32[512,512]{1,0:T(8,128)} collective-permute-done((f32[512,512]{1,0:T(8,128)S(1)}, f32[512,512]{1,0:T(8,128)}, u32[]{:S(2)}, u32[]{:S(2)}) %collective-permute-start.22) | collective-permute-done | bytes 1048608 | tf_op jit(solution)/shard_map/ppermute | solution.py:93
  1564.4 19.0 %collective-permute-done.24 = f32[512,512]{1,0:T(8,128)} collective-permute-done((f32[512,512]{1,0:T(8,128)S(1)}, f32[512,512]{1,0:T(8,128)}, u32[]{:S(2)}, u32[]{:S(2)}) %collective-permute-start.24) | collective-permute-done | bytes 1048608 | tf_op jit(solution)/shard_map/ppermute | solution.py:93
  1587.4 17.2 %collective-permute-done.25 = f32[512,512]{1,0:T(8,128)S(1)} collective-permute-done((f32[512,512]{1,0:T(8,128)S(1)}, f32[512,512]{1,0:T(8,128)S(1)}, u32[]{:S(2)}, u32[]{:S(2)}) %collective-permute-start.25) | collective-permute-done | bytes 1048608 | tf_op jit(solution)/shard_map/ppermute | solution.py:93
  1606.5 22.7 %collective-permute-done.28 = f32[512,512]{1,0:T(8,128)S(1)} collective-permute-done((f32[512,512]{1,0:T(8,128)S(1)}, f32[512,512]{1,0:T(8,128)S(1)}, u32[]{:S(2)}, u32[]{:S(2)}) %collective-permute-start.28) | collective-permute-done | bytes 1048608 | tf_op jit(solution)/shard_map/ppermute | solution.py:93
  1629.2 21.2 %collective-permute-done.29 = f32[512,512]{1,0:T(8,128)S(1)} collective-permute-done((f32[512,512]{1,0:T(8,128)S(1)}, f32[512,512]{1,0:T(8,128)S(1)}, u32[]{:S(2)}, u32[]{:S(2)}) %collective-permute-start.29) | collective-permute-done | bytes 1048608 | tf_op jit(solution)/shard_map/ppermute | solution.py:93
  (208 shorter events, 160.9 us)
Async XLA Ops:
  7.2 921.1 %all-gather.7.cloned.1.call-start = ((), (), s32[]{:S(2)}) async-start(), calls=%async_computation.1 | async-start | bytes 71303168 | tf_op jit(solution)/shard_map/all_gather | solution.py:31
  24.7 962.5 %all-gather.5.cloned.1.call-start = ((), (), s32[]{:S(2)}) async-start(), calls=%async_computation | async-start | bytes 71303168 | tf_op jit(solution)/shard_map/all_gather | solution.py:31
  344.3 339.1 %collective-permute-start = (f32[512,4096]{1,0:T(8,128)}, f32[512,4096]{1,0:T(8,128)}, u32[]{:S(2)}, u32[]{:S(2)}) collective-permute-start(f32[512,4096]{1,0:T(8,128)} %fusion.45), channel_id=1, source_target_pairs={{0,8},{8,0},{1,9},{9,1},{2,10},{10,2},{3,11},{11,3},{4,12},{12,4},... | collective-permute-start | bytes 25165832 | tf_op jit(solution)/shard_map/ppermute | solution.py:65
  430.6 432.6 %collective-permute-start.1 = (f32[512,4096]{1,0:T(8,128)}, f32[512,4096]{1,0:T(8,128)}, u32[]{:S(2)}, u32[]{:S(2)}) collective-permute-start(f32[512,4096]{1,0:T(8,128)} %fusion.51), channel_id=1, source_target_pairs={{0,8},{8,0},{1,9},{9,1},{2,10},{10,2},{3,11},{11,3},{4,12},{12,4},... | collective-permute-start | bytes 25165832 | tf_op jit(solution)/shard_map/ppermute | solution.py:65
  1189.7 142.7 %collective-permute-start.2 = (f32[512,512]{1,0:T(8,128)}, f32[512,512]{1,0:T(8,128)}, u32[]{:S(2)}, u32[]{:S(2)}) collective-permute-start(f32[512,512]{1,0:T(8,128)} %get-tuple-element.51), channel_id=1, source_target_pairs={{0,1},{1,0},{2,3},{3,2},{4,5},{5,4},{6,7},{7,6},{8,9},{9,8},{10,11... | collective-permute-start | bytes 3145736 | tf_op jit(solution)/shard_map/ppermute | solution.py:93
  1189.7 143.0 %collective-permute-start.3 = (f32[512,512]{1,0:T(8,128)}, f32[512,512]{1,0:T(8,128)}, u32[]{:S(2)}, u32[]{:S(2)}) collective-permute-start(f32[512,512]{1,0:T(8,128)} %get-tuple-element.52), channel_id=1, source_target_pairs={{0,2},{1,3},{2,0},{3,1},{4,6},{5,7},{6,4},{7,5},{8,10},{9,11},{10,... | collective-permute-start | bytes 3145736 | tf_op jit(solution)/shard_map/ppermute | solution.py:93
  1189.8 145.3 %collective-permute-start.4 = (f32[512,512]{1,0:T(8,128)}, f32[512,512]{1,0:T(8,128)}, u32[]{:S(2)}, u32[]{:S(2)}) collective-permute-start(f32[512,512]{1,0:T(8,128)} %get-tuple-element.53), channel_id=1, source_target_pairs={{0,3},{1,2},{2,1},{3,0},{4,7},{5,6},{6,5},{7,4},{8,11},{9,10},{10,... | collective-permute-start | bytes 3145736 | tf_op jit(solution)/shard_map/ppermute | solution.py:93
  1191.6 172.2 %collective-permute-start.5 = (f32[512,512]{1,0:T(8,128)}, f32[512,512]{1,0:T(8,128)}, u32[]{:S(2)}, u32[]{:S(2)}) collective-permute-start(f32[512,512]{1,0:T(8,128)} %get-tuple-element.54), channel_id=1, source_target_pairs={{0,4},{1,5},{2,6},{3,7},{4,0},{5,1},{6,2},{7,3},{8,12},{9,13},{10,... | collective-permute-start | bytes 3145736 | tf_op jit(solution)/shard_map/ppermute | solution.py:93
  1192.1 172.0 %collective-permute-start.6 = (f32[512,512]{1,0:T(8,128)}, f32[512,512]{1,0:T(8,128)}, u32[]{:S(2)}, u32[]{:S(2)}) collective-permute-start(f32[512,512]{1,0:T(8,128)} %get-tuple-element.55), channel_id=1, source_target_pairs={{0,5},{1,4},{2,7},{3,6},{4,1},{5,0},{6,3},{7,2},{8,13},{9,12},{10,... | collective-permute-start | bytes 3145736 | tf_op jit(solution)/shard_map/ppermute | solution.py:93
  1332.4 32.9 %collective-permute-start.7 = (f32[512,512]{1,0:T(8,128)S(1)}, f32[512,512]{1,0:T(8,128)}, u32[]{:S(2)}, u32[]{:S(2)}) collective-permute-start(f32[512,512]{1,0:T(8,128)S(1)} %copy-done.9), channel_id=1, source_target_pairs={{0,6},{1,7},{2,4},{3,5},{4,2},{5,3},{6,0},{7,1},{8,14},{9,15},{10,... | collective-permute-start | bytes 3145736 | tf_op jit(solution)/shard_map/ppermute | solution.py:93
  1332.7 48.1 %collective-permute-start.8 = (f32[512,512]{1,0:T(8,128)S(1)}, f32[512,512]{1,0:T(8,128)}, u32[]{:S(2)}, u32[]{:S(2)}) collective-permute-start(f32[512,512]{1,0:T(8,128)S(1)} %copy-done.8), channel_id=1, source_target_pairs={{0,7},{1,6},{2,5},{3,4},{4,3},{5,2},{6,1},{7,0},{8,15},{9,14},{10,... | collective-permute-start | bytes 3145736 | tf_op jit(solution)/shard_map/ppermute | solution.py:93
  1335.1 46.8 %collective-permute-start.9 = (f32[512,512]{1,0:T(8,128)}, f32[512,512]{1,0:T(8,128)}, u32[]{:S(2)}, u32[]{:S(2)}) collective-permute-start(f32[512,512]{1,0:T(8,128)} %get-tuple-element.59), channel_id=1, source_target_pairs={{0,1},{1,0},{2,3},{3,2},{4,5},{5,4},{6,7},{7,6},{8,9},{9,8},{10,11... | collective-permute-start | bytes 3145736 | tf_op jit(solution)/shard_map/ppermute | solution.py:93
  1363.8 39.7 %collective-permute-start.10 = (f32[512,512]{1,0:T(8,128)}, f32[512,512]{1,0:T(8,128)}, u32[]{:S(2)}, u32[]{:S(2)}) collective-permute-start(f32[512,512]{1,0:T(8,128)} %get-tuple-element.60), channel_id=1, source_target_pairs={{0,2},{1,3},{2,0},{3,1},{4,6},{5,7},{6,4},{7,5},{8,10},{9,11},{10,... | collective-permute-start | bytes 3145736 | tf_op jit(solution)/shard_map/ppermute | solution.py:93
  1364.1 60.9 %collective-permute-start.11 = (f32[512,512]{1,0:T(8,128)}, f32[512,512]{1,0:T(8,128)}, u32[]{:S(2)}, u32[]{:S(2)}) collective-permute-start(f32[512,512]{1,0:T(8,128)} %get-tuple-element.61), channel_id=1, source_target_pairs={{0,3},{1,2},{2,1},{3,0},{4,7},{5,6},{6,5},{7,4},{8,11},{9,10},{10,... | collective-permute-start | bytes 3145736 | tf_op jit(solution)/shard_map/ppermute | solution.py:93
  1365.3 62.0 %collective-permute-start.12 = (f32[512,512]{1,0:T(8,128)}, f32[512,512]{1,0:T(8,128)}, u32[]{:S(2)}, u32[]{:S(2)}) collective-permute-start(f32[512,512]{1,0:T(8,128)} %get-tuple-element.62), channel_id=1, source_target_pairs={{0,4},{1,5},{2,6},{3,7},{4,0},{5,1},{6,2},{7,3},{8,12},{9,13},{10,... | collective-permute-start | bytes 3145736 | tf_op jit(solution)/shard_map/ppermute | solution.py:93
  1380.8 48.2 %collective-permute-start.13 = (f32[512,512]{1,0:T(8,128)}, f32[512,512]{1,0:T(8,128)}, u32[]{:S(2)}, u32[]{:S(2)}) collective-permute-start(f32[512,512]{1,0:T(8,128)} %get-tuple-element.63), channel_id=1, source_target_pairs={{0,5},{1,4},{2,7},{3,6},{4,1},{5,0},{6,3},{7,2},{8,13},{9,12},{10,... | collective-permute-start | bytes 3145736 | tf_op jit(solution)/shard_map/ppermute | solution.py:93
  1381.9 67.5 %collective-permute-start.14 = (f32[512,512]{1,0:T(8,128)}, f32[512,512]{1,0:T(8,128)}, u32[]{:S(2)}, u32[]{:S(2)}) collective-permute-start(f32[512,512]{1,0:T(8,128)} %get-tuple-element.64), channel_id=1, source_target_pairs={{0,6},{1,7},{2,4},{3,5},{4,2},{5,3},{6,0},{7,1},{8,14},{9,15},{10,... | collective-permute-start | bytes 3145736 | tf_op jit(solution)/shard_map/ppermute | solution.py:93
  1403.5 67.2 %collective-permute-start.15 = (f32[512,512]{1,0:T(8,128)}, f32[512,512]{1,0:T(8,128)S(1)}, u32[]{:S(2)}, u32[]{:S(2)}) collective-permute-start(f32[512,512]{1,0:T(8,128)} %get-tuple-element.65), channel_id=1, source_target_pairs={{0,7},{1,6},{2,5},{3,4},{4,3},{5,2},{6,1},{7,0},{8,15},{9,14},{10,... | collective-permute-start | bytes 3145736 | tf_op jit(solution)/shard_map/ppermute | solution.py:93
  1424.9 48.1 %collective-permute-start.16 = (f32[512,512]{1,0:T(8,128)}, f32[512,512]{1,0:T(8,128)S(1)}, u32[]{:S(2)}, u32[]{:S(2)}) collective-permute-start(f32[512,512]{1,0:T(8,128)} %get-tuple-element.67), channel_id=1, source_target_pairs={{0,1},{1,0},{2,3},{3,2},{4,5},{5,4},{6,7},{7,6},{8,9},{9,8},{10,11... | collective-permute-start | bytes 3145736 | tf_op jit(solution)/shard_map/ppermute | solution.py:93
  1427.4 65.9 %collective-permute-start.17 = (f32[512,512]{1,0:T(8,128)}, f32[512,512]{1,0:T(8,128)S(1)}, u32[]{:S(2)}, u32[]{:S(2)}) collective-permute-start(f32[512,512]{1,0:T(8,128)} %get-tuple-element.68), channel_id=1, source_target_pairs={{0,2},{1,3},{2,0},{3,1},{4,6},{5,7},{6,4},{7,5},{8,10},{9,11},{10,... | collective-permute-start | bytes 3145736 | tf_op jit(solution)/shard_map/ppermute | solution.py:93
  1429.1 85.7 %collective-permute-start.18 = (f32[512,512]{1,0:T(8,128)}, f32[512,512]{1,0:T(8,128)S(1)}, u32[]{:S(2)}, u32[]{:S(2)}) collective-permute-start(f32[512,512]{1,0:T(8,128)} %get-tuple-element.69), channel_id=1, source_target_pairs={{0,3},{1,2},{2,1},{3,0},{4,7},{5,6},{6,5},{7,4},{8,11},{9,10},{10,... | collective-permute-start | bytes 3145736 | tf_op jit(solution)/shard_map/ppermute | solution.py:93
  1449.4 67.8 %collective-permute-start.19 = (f32[512,512]{1,0:T(8,128)}, f32[512,512]{1,0:T(8,128)}, u32[]{:S(2)}, u32[]{:S(2)}) collective-permute-start(f32[512,512]{1,0:T(8,128)} %get-tuple-element.70), channel_id=1, source_target_pairs={{0,4},{1,5},{2,6},{3,7},{4,0},{5,1},{6,2},{7,3},{8,12},{9,13},{10,... | collective-permute-start | bytes 3145736 | tf_op jit(solution)/shard_map/ppermute | solution.py:93
  1470.7 47.2 %collective-permute-start.20 = (f32[512,512]{1,0:T(8,128)S(1)}, f32[512,512]{1,0:T(8,128)S(1)}, u32[]{:S(2)}, u32[]{:S(2)}) collective-permute-start(f32[512,512]{1,0:T(8,128)S(1)} %copy-done.7), channel_id=1, source_target_pairs={{0,5},{1,4},{2,7},{3,6},{4,1},{5,0},{6,3},{7,2},{8,13},{9,12},{10,... | collective-permute-start | bytes 3145736 | tf_op jit(solution)/shard_map/ppermute | solution.py:93
  1473.0 66.3 %collective-permute-start.21 = (f32[512,512]{1,0:T(8,128)S(1)}, f32[512,512]{1,0:T(8,128)}, u32[]{:S(2)}, u32[]{:S(2)}) collective-permute-start(f32[512,512]{1,0:T(8,128)S(1)} %get-tuple-element.72), channel_id=1, source_target_pairs={{0,6},{1,7},{2,4},{3,5},{4,2},{5,3},{6,0},{7,1},{8,14},{9,15},{10,... | collective-permute-start | bytes 3145736 | tf_op jit(solution)/shard_map/ppermute | solution.py:93
  1493.3 67.4 %collective-permute-start.22 = (f32[512,512]{1,0:T(8,128)S(1)}, f32[512,512]{1,0:T(8,128)}, u32[]{:S(2)}, u32[]{:S(2)}) collective-permute-start(f32[512,512]{1,0:T(8,128)S(1)} %get-tuple-element.73), channel_id=1, source_target_pairs={{0,7},{1,6},{2,5},{3,4},{4,3},{5,2},{6,1},{7,0},{8,15},{9,14},{10,... | collective-permute-start | bytes 3145736 | tf_op jit(solution)/shard_map/ppermute | solution.py:93
  1514.8 47.0 %collective-permute-start.23 = (f32[512,512]{1,0:T(8,128)S(1)}, f32[512,512]{1,0:T(8,128)}, u32[]{:S(2)}, u32[]{:S(2)}) collective-permute-start(f32[512,512]{1,0:T(8,128)S(1)} %get-tuple-element.75), channel_id=1, source_target_pairs={{0,1},{1,0},{2,3},{3,2},{4,5},{5,4},{6,7},{7,6},{8,9},{9,8},{10,11... | collective-permute-start | bytes 3145736 | tf_op jit(solution)/shard_map/ppermute | solution.py:93
  1517.2 66.1 %collective-permute-start.24 = (f32[512,512]{1,0:T(8,128)S(1)}, f32[512,512]{1,0:T(8,128)}, u32[]{:S(2)}, u32[]{:S(2)}) collective-permute-start(f32[512,512]{1,0:T(8,128)S(1)} %get-tuple-element.76), channel_id=1, source_target_pairs={{0,2},{1,3},{2,0},{3,1},{4,6},{5,7},{6,4},{7,5},{8,10},{9,11},{10,... | collective-permute-start | bytes 3145736 | tf_op jit(solution)/shard_map/ppermute | solution.py:93
  1517.9 86.8 %collective-permute-start.25 = (f32[512,512]{1,0:T(8,128)S(1)}, f32[512,512]{1,0:T(8,128)S(1)}, u32[]{:S(2)}, u32[]{:S(2)}) collective-permute-start(f32[512,512]{1,0:T(8,128)S(1)} %get-tuple-element.77), channel_id=1, source_target_pairs={{0,3},{1,2},{2,1},{3,0},{4,7},{5,6},{6,5},{7,4},{8,11},{9,10},{10,... | collective-permute-start | bytes 3145736 | tf_op jit(solution)/shard_map/ppermute | solution.py:93
  1539.3 65.5 %collective-permute-start.26 = (f32[512,512]{1,0:T(8,128)S(1)}, f32[512,512]{1,0:T(8,128)S(1)}, u32[]{:S(2)}, u32[]{:S(2)}) collective-permute-start(f32[512,512]{1,0:T(8,128)S(1)} %get-tuple-element.78), channel_id=1, source_target_pairs={{0,4},{1,5},{2,6},{3,7},{4,0},{5,1},{6,2},{7,3},{8,12},{9,13},{10,... | collective-permute-start | bytes 3145736 | tf_op jit(solution)/shard_map/ppermute | solution.py:93
  1560.7 45.7 %collective-permute-start.27 = (f32[512,512]{1,0:T(8,128)S(1)}, f32[512,512]{1,0:T(8,128)S(1)}, u32[]{:S(2)}, u32[]{:S(2)}) collective-permute-start(f32[512,512]{1,0:T(8,128)S(1)} %get-tuple-element.79), channel_id=1, source_target_pairs={{0,5},{1,4},{2,7},{3,6},{4,1},{5,0},{6,3},{7,2},{8,13},{9,12},{10,... | collective-permute-start | bytes 3145736 | tf_op jit(solution)/shard_map/ppermute | solution.py:93
  1561.8 67.3 %collective-permute-start.28 = (f32[512,512]{1,0:T(8,128)S(1)}, f32[512,512]{1,0:T(8,128)S(1)}, u32[]{:S(2)}, u32[]{:S(2)}) collective-permute-start(f32[512,512]{1,0:T(8,128)S(1)} %get-tuple-element.80), channel_id=1, source_target_pairs={{0,6},{1,7},{2,4},{3,5},{4,2},{5,3},{6,0},{7,1},{8,14},{9,15},{10,... | collective-permute-start | bytes 3145736 | tf_op jit(solution)/shard_map/ppermute | solution.py:93
  1583.3 67.1 %collective-permute-start.29 = (f32[512,512]{1,0:T(8,128)S(1)}, f32[512,512]{1,0:T(8,128)S(1)}, u32[]{:S(2)}, u32[]{:S(2)}) collective-permute-start(f32[512,512]{1,0:T(8,128)S(1)} %get-tuple-element.81), channel_id=1, source_target_pairs={{0,7},{1,6},{2,5},{3,4},{4,3},{5,2},{6,1},{7,0},{8,15},{9,14},{10,... | collective-permute-start | bytes 3145736 | tf_op jit(solution)/shard_map/ppermute | solution.py:93
  (35 other events, 4206.0 us)
Sparse Core Ops, SparseCore 0:
  24.8 246.5 all-gather.6
  273.7 398.5 all-gather.4

commit v2 on v1

--- a/solution.py
+++ b/solution.py
@@ -59,10 +59,19 @@
         own_row_w = lax.dynamic_index_in_dim(all_row_w, dp_rank, 0, keepdims=False).reshape(2 * rows)
         probs = jnp.exp(logits - own_lse[:, None])
         grad_z = (own_row_w[:, None] * jnp.where(is_target, probs - 1.0, probs)).astype(jnp.bfloat16)
-        grad_u = []
+        grad_u, gain_parts = [], []
         for which in range(2):
             part = lax.dot_general(grad_z[which * rows:(which + 1) * rows], w_out, (((1,), (1,)), ((), ())), preferred_element_type=jnp.float32).astype(jnp.bfloat16).astype(jnp.float32)
+            h, part = lax.optimization_barrier(((h_main, h_mtp)[which], part))
+            x = h.reshape(rows, d_model).astype(jnp.float32)
+            gain_parts.append(jnp.sum(part * (x * lax.rsqrt(jnp.mean(x * x, axis=-1, keepdims=True) + NORM_EPS)), axis=0))
             grad_u.append((part, lax.ppermute(part, 'tp', [(i, n_tp - 1 - i) for i in range(n_tp)])))
+        grad_gain = jnp.stack(gain_parts)
+        for axis, size in (('dp', n_dp), ('tp', n_tp)):
+            bit = 1
+            while bit < size:
+                grad_gain = grad_gain + lax.ppermute(grad_gain, axis, [(i, i ^ bit) for i in range(size)])
+                bit *= 2
 
         width = -(-shard_vocab // (n_dp * 256)) * 256
         col_unit = jnp.minimum(dp_rank * (width // 256), (shard_vocab - width) // 256)
@@ -80,13 +89,13 @@
             return lax.dot_general(u_all, e, (((0,), (0,)), ((), ())), preferred_element_type=jnp.float32)
 
         u_all = [(n * g).astype(jnp.bfloat16) for n, g in zip(gathered, gains)]
-        grad_main = slice_grad(0, u_all[0], w_slice, slice_start)
         d_loc = d_model // n_dp
         grad_w = jnp.zeros((d_loc, shard_vocab), jnp.float32)
         cw = width // CHUNKS
         for q in range(CHUNKS):
             cols = w_slice[:, q * cw:(q + 1) * cw]
-            part = grad_main[:, q * cw:(q + 1) * cw] + slice_grad(1, u_all[1], cols, slice_start + q * cw)
+            part = slice_grad(0, u_all[0], cols, slice_start + q * cw)
+            part = part + slice_grad(1, u_all[1], cols, slice_start + q * cw)
             sends = lax.optimization_barrier([lax.dynamic_slice(part, ((dp_rank ^ k) * d_loc, 0), (d_loc, cw)) for k in range(n_dp)])
             for k, block in enumerate(sends):
                 if k:
@@ -94,7 +103,7 @@
                 peer_unit = jnp.minimum((dp_rank ^ k) * (width // 256), (shard_vocab - width) // 256)
                 grad_w = lax.dynamic_update_slice(grad_w, block, (0, (peer_unit + q * cw // 256) * 256))
 
-        grads_h, gain_parts = [], []
+        grads_h = []
         for which, h in enumerate((h_main, h_mtp)):
             h, part, other = lax.optimization_barrier((h, *grad_u[which]))
             x = h.reshape(rows, d_model).astype(jnp.float32)
@@ -102,12 +111,9 @@
             n = x * inv
             du = part + other
             grad_normed = du * gains[which]
-            gain_parts.append(jnp.sum(du * n, axis=0))
             grad_x = inv * (grad_normed - n * jnp.mean(grad_normed * n, axis=-1, keepdims=True))
             grads_h.append(grad_x.astype(jnp.bfloat16).reshape(batch_loc, seq_len, d_model))
-        grad_gain = lax.psum(jnp.stack(gain_parts), 'dp')
         return loss_total, grads_h[0], grads_h[1], grad_w, grad_gain[0], grad_gain[1]
-
 
     row_spec = P('dp', None)
     return jax.shard_map(layer_step, mesh=mesh, in_specs=(P('dp', None, None), P('dp', None, None), row_spec, row_spec, row_spec, row_spec, P(None), P(None), P(None, 'tp')), out_specs=(P(), P('dp', None, None), P('dp', None, None), P('dp', 'tp'), P(None), P(None)), check_vma=False)

time: 1680 us -> 1740 us (1.036)
  other arithmetic: 151 us -> 192 us
  matrix products: 705 us -> 740 us
  blocking collectives: 41.5 us -> 17.6 us
    ppermute x2, waiting for transfers between devices: 430 us -> 0.01 us  [layer_step(): lax.ppermute(part, 'tp', [(i, n_tp - 1 - i) for i in range(n_tp)])]
    ppermute x0 -> x4, waiting for transfers between devices: none -> 405 us  [layer_step(): lax.ppermute(grad_gain, axis, [(i, i ^ bit) for i in range(size)])]
    convert_element_type x1 -> x2, other arithmetic: 32.7 us -> 65.4 us  [layer_step(): u_all = [(n * g).astype(jnp.bfloat16) for n, g in zip(gathered, gains)]]
    psum x1 -> x0, blocking collectives: 24.2 us -> none  [layer_step(): grad_gain = lax.psum(jnp.stack(gain_parts), 'dp')]
    dot_general x5 -> x8, matrix products: 190 us -> 210 us  [slice_grad(): z = jnp.dot(u_all, cols, preferred_element_type=jnp.float32)]
    dot_general x5 -> x8, matrix products: 196 us -> 211 us  [slice_grad(): lax.dot_general(u_all, e, (((0,), (0,)), ((), ())), preferred_element_typ...]
  transfers between devices with their start and end apart: 32 -> 36, of which waited for: 16 -> 14; matrix products, arithmetic and copies ran while one was open for 41% -> 35% of each run, Pallas kernels for 0% -> 0%
where the time goes in v2:
time: 1740 us
  matrix products  740 us (43%)
  waiting for transfers between devices  657 us (38%)
  other arithmetic  192 us (11%)
  local copies, waits for them, and re-layouts  73.5 us (4%)
  starting transfers between devices  39.1 us (2%)
  blocking collectives  17.6 us (1%)
    ppermute x4, waiting for transfers between devices, layer_step(): lax.ppermute(grad_gain, axis, [(i, i ^ bit) for i in range(size)])  405 us
    ppermute x28, waiting for transfers between devices, layer_step(): block = lax.ppermute(block, 'dp', [(i, i ^ k) for i in range(n_dp)])  252 us
    dot_general x8, matrix products, slice_grad(): lax.dot_general(u_all, e, (((0,), (0,)), ((), ())), preferred_element_typ...  211 us
    dot_general x8, matrix products, slice_grad(): z = jnp.dot(u_all, cols, preferred_element_type=jnp.float32)  210 us
    dot_general x2, matrix products, layer_step(): lax.dot_general(grad_z[which * rows:(which + 1) * rows], w_out, (((1,), (...  166 us
    dot_general x1, matrix products, layer_step(): logits = jnp.dot(u_rows, w_out, preferred_element_type=jnp.float32)  153 us
    convert_element_type x2, other arithmetic, layer_step(): u_all = [(n * g).astype(jnp.bfloat16) for n, g in zip(gathered, gains)]  65.4 us
  transfers between devices with their start and end apart: 36, of which 14 were waited for; matrix products, arithmetic and copies ran while one was open for 35% of the time, Pallas kernels for 0%

profile of v2, /device:TPU:0, one launch (start us, length us, event | category | flops | bytes accessed | tf_op | source)
XLA Modules:
  0.0 1735.0 jit_solution(13513201755802994260)
XLA Ops:
  31.6 153.3 %fusion.109 = (f32[1024]{0:T(1024)S(1)}, f32[1024,16128]{1,0:T(8,128)}) fusion(bf16[4096,16128]{1,0:T(8,128)(2,1)} %param.18, bf16[512,4096]{1,0:T(8,128)(2,1)} %get-tuple-element.136, bf16[512,4096]{1,0:T(8,128)(2,1)} %get-tuple-element.143), kind=kOutput, calls=%fused_computation.222 | convolution fusion | flops 135324762112 | bytes 206573568 | tf_op jit(solution)/shard_map/dot_general | solution.py:40
  184.9 24.7 %select_reduce_fusion = (f32[1024]{0:T(1024)S(1)}, f32[1024]{0:T(1024)S(1)}) fusion(f32[1024,16128]{1,0:T(8,128)} %get-tuple-element.142, s32[1024]{0:T(1024)S(1)} %copy-done.24, f32[1024]{0:T(1024)S(1)} %get-tuple-element.141), kind=kLoop, calls=%fused_computation.5 | loop fusion | flops 82573312 | bytes 66076672 | tf_op jit(solution)/shard_map/reduce_sum | solution.py:44
  209.7 17.6 %all-gather.1 = f32[16,5,1024]{2,1,0:T(8,128)S(1)} all-gather(f32[1,5,1024]{2,1,0:T(8,128)S(1)} %bitcast.168), channel_id=2, replica_groups=mesh['tp'=2,'dp'=8] {'tp','dp'}, dimensions={0}, use_global_device_ids=true | all-gather | bytes 348160 | tf_op jit(solution)/shard_map/all_gather | solution.py:47
  229.2 33.6 %fusion.1 = bf16[1024,16128]{1,0:T(8,128)(2,1)} fusion(f32[1024,16128]{1,0:T(8,128)} %get-tuple-element.142, f32[1024]{0:T(1024)S(1)} %bitcast.176, f32[1024]{0:T(1024)S(1)} %bitcast.175, s32[1024]{0:T(1024)S(1)} %copy-done.24), kind=kLoop, calls=%fused_computation.4 | loop fusion | flops 99090432 | bytes 99102720 | tf_op jit(solution)/shard_map/convert_element_type | solution.py:61
  262.8 82.8 %fusion.57 = f32[512,4096]{1,0:T(8,128)} fusion(bf16[4096,16128]{1,0:T(8,128)(2,1)} %param.18, bf16[1024,16128]{1,0:T(8,128)(2,1)} %fusion.1), kind=kOutput, calls=%fused_computation.85 | convolution fusion | flops 67649929216 | bytes 157024256 | tf_op jit(solution)/shard_map/dot_general | solution.py:64
  348.1 83.4 %fusion.51 = f32[512,4096]{1,0:T(8,128)} fusion(bf16[4096,16128]{1,0:T(8,128)(2,1)} %param.18, bf16[1024,16128]{1,0:T(8,128)(2,1)} %fusion.1), kind=kOutput, calls=%fused_computation.83 | convolution fusion | flops 67649929216 | bytes 157024256 | tf_op jit(solution)/shard_map/dot_general | solution.py:64
  465.6 398.6 %collective-permute-done.33 = f32[2,4096]{1,0:T(2,128)S(1)} collective-permute-done((f32[2,4096]{1,0:T(2,128)S(1)}, f32[2,4096]{1,0:T(2,128)S(1)}, u32[]{:S(2)}, u32[]{:S(2)}) %collective-permute-start.33) | collective-permute-done | bytes 32800 | tf_op jit(solution)/shard_map/ppermute | solution.py:73
  898.3 32.7 %multiply_convert_fusion.1 = bf16[4096,4096]{1,0:T(8,128)(2,1)} fusion(f32[4096,4096]{1,0:T(8,128)} %all-gather.5.cloned.1.call-done, f32[4096]{0:T(1024)S(1)} %copy-done.17), kind=kLoop, calls=%fused_computation.2 | loop fusion | flops 33554432 | bytes 100679680 | tf_op jit(solution)/shard_map/convert_element_type | solution.py:91
  931.0 26.2 %fusion.41.clone.4 = bf16[4096,512]{1,0:T(8,128)(2,1)} fusion(bf16[4096,4096]{1,0:T(8,128)(2,1)} %multiply_convert_fusion.1, s32[512]{0:T(512)S(1)} %iota_add_fusion, f32[4096]{0:T(1024)S(1)} %bitcast.184, f32[4096]{0:T(1024)S(1)} %bitcast.180, s32[4096]{0:T(1024)S(1)} %bitcast.188, bf16[4096,16128]{1,0:T(8,128)(2,1)} %param.18, ...), kind=kOutput, calls=%fused_computation.67.clone.clone.clone.1 | convolution fusion | flops 17192452096 | bytes 41994244 | tf_op jit(solution)/shard_map/dot_general | solution.py:85
  957.2 26.5 %fusion.37.clone.2 = bf16[4096,512]{1,0:T(8,128)(2,1)} fusion(bf16[4096,4096]{1,0:T(8,128)(2,1)} %multiply_convert_fusion.1, s32[512]{0:T(512)S(1)} %iota_add_fusion.1, f32[4096]{0:T(1024)S(1)} %bitcast.185, f32[4096]{0:T(1024)S(1)} %bitcast.181, s32[4096]{0:T(1024)S(1)} %bitcast.189, bf16[4096,16128]{1,0:T(8,128)(2,1)} %param.18, ...), kind=kOutput, calls=%fused_computation.63.clone.clone.clone | convolution fusion | flops 17192452096 | bytes 41994244 | tf_op jit(solution)/shard_map/dot_general | solution.py:85
  983.7 32.7 %multiply_convert_fusion = bf16[4096,4096]{1,0:T(8,128)(2,1)} fusion(f32[4096,4096]{1,0:T(8,128)} %all-gather.7.cloned.1.call-done, f32[4096]{0:T(1024)S(1)} %copy-done.19), kind=kLoop, calls=%fused_computation.1 | loop fusion | flops 33554432 | bytes 100679680 | tf_op jit(solution)/shard_map/convert_element_type | solution.py:91
  1016.5 26.1 %fusion.43 = bf16[4096,512]{1,0:T(8,128)(2,1)} fusion(bf16[4096,4096]{1,0:T(8,128)(2,1)} %multiply_convert_fusion, s32[512]{0:T(512)S(1)} %iota_add_fusion, f32[4096]{0:T(1024)S(1)} %bitcast.196, f32[4096]{0:T(1024)S(1)} %bitcast.192, s32[4096]{0:T(1024)S(1)} %bitcast.200, bf16[4096,16128]{1,0:T(8,128)(2,1)} %param.18, s32[]{:T(128)S(6)} %add.488), kind=kOutput, calls=%fused_computation.69 | convolution fusion | flops 17192452096 | bytes 41994244 | tf_op jit(solution)/shard_map/dot_general | solution.py:85
  1042.6 26.2 %fusion.39 = bf16[4096,512]{1,0:T(8,128)(2,1)} fusion(bf16[4096,4096]{1,0:T(8,128)(2,1)} %multiply_convert_fusion, s32[512]{0:T(512)S(1)} %iota_add_fusion.1, f32[4096]{0:T(1024)S(1)} %bitcast.197, f32[4096]{0:T(1024)S(1)} %bitcast.193, s32[4096]{0:T(1024)S(1)} %bitcast.201, bf16[4096,16128]{1,0:T(8,128)(2,1)} %param.18, s32[]{:T(128)S(6)} %add.487), kind=kOutput, calls=%fused_computation.65 | convolution fusion | flops 17192452096 | bytes 41994244 | tf_op jit(solution)/shard_map/dot_general | solution.py:85
  1068.8 26.1 %fusion.33.clone.2 = bf16[4096,512]{1,0:T(8,128)(2,1)} fusion(bf16[4096,4096]{1,0:T(8,128)(2,1)} %multiply_convert_fusion.1, s32[512]{0:T(512)S(1)} %copy-done.33, f32[4096]{0:T(1024)S(1)} %bitcast.186, f32[4096]{0:T(1024)S(1)} %bitcast.182, s32[4096]{0:T(1024)S(1)} %bitcast.190, bf16[4096,16128]{1,0:T(8,128)(2,1)} %param.18, s32[]{:T(128)S(6)} %add.486), kind=kOutput, calls=%fused_computation.59.clone.clone.clone | convolution fusion | flops 17192452096 | bytes 41994244 | tf_op jit(solution)/shard_map/dot_general | solution.py:85
  1094.9 26.4 %fusion.35 = bf16[4096,512]{1,0:T(8,128)(2,1)} fusion(bf16[4096,4096]{1,0:T(8,128)(2,1)} %multiply_convert_fusion, s32[512]{0:T(512)S(1)} %copy-done.33, f32[4096]{0:T(1024)S(1)} %bitcast.198, f32[4096]{0:T(1024)S(1)} %bitcast.194, s32[4096]{0:T(1024)S(1)} %bitcast.202, bf16[4096,16128]{1,0:T(8,128)(2,1)} %param.18, s32[]{:T(128)S(6)} %add.486), kind=kOutput, calls=%fused_computation.61 | convolution fusion | flops 17192452096 | bytes 41994244 | tf_op jit(solution)/shard_map/dot_general | solution.py:85
  1121.4 26.1 %fusion.31 = bf16[4096,512]{1,0:T(8,128)(2,1)} fusion(bf16[4096,4096]{1,0:T(8,128)(2,1)} %multiply_convert_fusion, f32[4096]{0:T(1024)S(1)} %bitcast.199, f32[4096]{0:T(1024)S(1)} %bitcast.195, s32[512]{0:T(512)S(1)} %copy-done.32, s32[4096]{0:T(1024)S(1)} %bitcast.203, bf16[4096,16128]{1,0:T(8,128)(2,1)} %param.18, s32[]{:T(128)S(6)} %select_n.191), kind=kOutput, calls=%fused_computation.57 | convolution fusion | flops 17192452096 | bytes 41994244 | tf_op jit(solution)/shard_map/dot_general | solution.py:85
  1147.4 26.6 %fusion.29.clone.4 = bf16[4096,512]{1,0:T(8,128)(2,1)} fusion(bf16[4096,4096]{1,0:T(8,128)(2,1)} %multiply_convert_fusion.1, f32[4096]{0:T(1024)S(1)} %bitcast.187, s32[512]{0:T(512)S(1)} %copy-done.32, f32[4096]{0:T(1024)S(1)} %bitcast.183, s32[4096]{0:T(1024)S(1)} %bitcast.191, bf16[4096,16128]{1,0:T(8,128)(2,1)} %param.18, ...), kind=kOutput, calls=%fused_computation.55.clone.clone.clone.1 | convolution fusion | flops 17192452096 | bytes 41994244 | tf_op jit(solution)/shard_map/dot_general | solution.py:85
  1174.1 24.4 %fusion.65 = f32[4096,512]{1,0:T(8,128)} fusion(bf16[4096,4096]{1,0:T(8,128)(2,1)} %multiply_convert_fusion.1, bf16[4096,512]{1,0:T(8,128)(2,1)S(1)} %copy-done.38), kind=kOutput, calls=%fused_computation.90 | convolution fusion | flops 17179869184 | bytes 46137344 | tf_op jit(solution)/shard_map/dot_general | solution.py:89
  1198.5 24.7 %fusion.70 = f32[4096,512]{1,0:T(8,128)} fusion(bf16[4096,4096]{1,0:T(8,128)(2,1)} %multiply_convert_fusion.1, bf16[4096,512]{1,0:T(8,128)(2,1)S(1)} %copy-done.37), kind=kOutput, calls=%fused_computation.93 | convolution fusion | flops 17179869184 | bytes 46137344 | tf_op jit(solution)/shard_map/dot_general | solution.py:89
  1223.2 24.3 %fusion.75 = f32[4096,512]{1,0:T(8,128)} fusion(bf16[4096,4096]{1,0:T(8,128)(2,1)} %multiply_convert_fusion.1, bf16[4096,512]{1,0:T(8,128)(2,1)S(1)} %copy-done.40), kind=kOutput, calls=%fused_computation.96 | convolution fusion | flops 17179869184 | bytes 46137344 | tf_op jit(solution)/shard_map/dot_general | solution.py:89
  1247.5 28.2 %convolution_add_fusion.2 = f32[4096,512]{1,0:T(8,128)} fusion(f32[4096,512]{1,0:T(8,128)} %fusion.75, bf16[4096,4096]{1,0:T(8,128)(2,1)} %multiply_convert_fusion, bf16[4096,512]{1,0:T(8,128)(2,1)} %fusion.35), kind=kOutput, calls=%fused_computation.80 | convolution fusion | flops 17181966336 | bytes 54525952 | tf_op jit(solution)/shard_map/dot_general | solution.py:89
  1282.7 24.3 %fusion.80 = f32[4096,512]{1,0:T(8,128)} fusion(bf16[4096,4096]{1,0:T(8,128)(2,1)} %multiply_convert_fusion.1, bf16[4096,512]{1,0:T(8,128)(2,1)S(1)} %copy-done.39), kind=kOutput, calls=%fused_computation.99 | convolution fusion | flops 17179869184 | bytes 46137344 | tf_op jit(solution)/shard_map/dot_general | solution.py:89
  1307.0 28.4 %convolution_add_fusion.3 = f32[4096,512]{1,0:T(8,128)} fusion(f32[4096,512]{1,0:T(8,128)} %fusion.80, bf16[4096,4096]{1,0:T(8,128)(2,1)} %multiply_convert_fusion, bf16[4096,512]{1,0:T(8,128)(2,1)} %fusion.31), kind=kOutput, calls=%fused_computation.81 | convolution fusion | flops 17181966336 | bytes 54525952 | tf_op jit(solution)/shard_map/dot_general | solution.py:89
  1345.4 28.2 %convolution_add_fusion = f32[4096,512]{1,0:T(8,128)} fusion(f32[4096,512]{1,0:T(8,128)} %fusion.65, bf16[4096,4096]{1,0:T(8,128)(2,1)} %multiply_convert_fusion, bf16[4096,512]{1,0:T(8,128)(2,1)} %fusion.43), kind=kOutput, calls=%fused_computation.78 | convolution fusion | flops 17181966336 | bytes 54525952 | tf_op jit(solution)/shard_map/dot_general | solution.py:89
  1390.7 28.2 %convolution_add_fusion.1 = f32[4096,512]{1,0:T(8,128)} fusion(f32[4096,512]{1,0:T(8,128)} %fusion.70, bf16[4096,4096]{1,0:T(8,128)(2,1)} %multiply_convert_fusion, bf16[4096,512]{1,0:T(8,128)(2,1)} %fusion.39), kind=kOutput, calls=%fused_computation.79 | convolution fusion | flops 17181966336 | bytes 54525952 | tf_op jit(solution)/shard_map/dot_general | solution.py:89
  1420.5 15.5 collective-permute-done.6
  1460.4 19.2 %collective-permute-done.11 = f32[512,512]{1,0:T(8,128)} collective-permute-done((f32[512,512]{1,0:T(8,128)}, f32[512,512]{1,0:T(8,128)}, u32[]{:S(2)}, u32[]{:S(2)}) %collective-permute-start.11) | collective-permute-done | bytes 1048608 | tf_op jit(solution)/shard_map/ppermute | solution.py:102
  1484.8 44.6 %collective-permute-done.13 = f32[512,512]{1,0:T(8,128)} collective-permute-done((f32[512,512]{1,0:T(8,128)S(1)}, f32[512,512]{1,0:T(8,128)}, u32[]{:S(2)}, u32[]{:S(2)}) %collective-permute-start.13) | collective-permute-done | bytes 1048608 | tf_op jit(solution)/shard_map/ppermute | solution.py:102
  1550.3 19.2 %collective-permute-done.18 = f32[512,512]{1,0:T(8,128)S(1)} collective-permute-done((f32[512,512]{1,0:T(8,128)}, f32[512,512]{1,0:T(8,128)S(1)}, u32[]{:S(2)}, u32[]{:S(2)}) %collective-permute-start.18) | collective-permute-done | bytes 1048608 | tf_op jit(solution)/shard_map/ppermute | solution.py:102
  1577.3 46.1 %collective-permute-done.20 = f32[512,512]{1,0:T(8,128)S(1)} collective-permute-done((f32[512,512]{1,0:T(8,128)S(1)}, f32[512,512]{1,0:T(8,128)S(1)}, u32[]{:S(2)}, u32[]{:S(2)}) %collective-permute-start.20) | collective-permute-done | bytes 1048608 | tf_op jit(solution)/shard_map/ppermute | solution.py:102
  1641.6 17.7 %collective-permute-done.25 = f32[512,512]{1,0:T(8,128)S(1)} collective-permute-done((f32[512,512]{1,0:T(8,128)S(1)}, f32[512,512]{1,0:T(8,128)S(1)}, u32[]{:S(2)}, u32[]{:S(2)}) %collective-permute-start.25) | collective-permute-done | bytes 1048608 | tf_op jit(solution)/shard_map/ppermute | solution.py:102
  1659.5 56.7 %collective-permute-done.27 = f32[512,512]{1,0:T(8,128)S(1)} collective-permute-done((f32[512,512]{1,0:T(8,128)S(1)}, f32[512,512]{1,0:T(8,128)S(1)}, u32[]{:S(2)}, u32[]{:S(2)}) %collective-permute-start.27) | collective-permute-done | bytes 1048608 | tf_op jit(solution)/shard_map/ppermute | solution.py:102
  (252 shorter events, 220.8 us)
Async XLA Ops:
  7.2 891.1 %all-gather.5.cloned.1.call-start = ((), (), s32[]{:S(2)}) async-start(), calls=%async_computation | async-start | bytes 71303168 | tf_op jit(solution)/shard_map/all_gather | solution.py:31
  25.1 958.7 %all-gather.7.cloned.1.call-start = ((), (), s32[]{:S(2)}) async-start(), calls=%async_computation.1 | async-start | bytes 71303168 | tf_op jit(solution)/shard_map/all_gather | solution.py:31
  345.6 519.2 %collective-permute-start.1 = (f32[512,4096]{1,0:T(8,128)}, f32[512,4096]{1,0:T(8,128)}, u32[]{:S(2)}, u32[]{:S(2)}) collective-permute-start(f32[512,4096]{1,0:T(8,128)} %fusion.57), channel_id=1, source_target_pairs={{0,8},{8,0},{1,9},{9,1},{2,10},{10,2},{3,11},{11,3},{4,12},{12,4},... | collective-permute-start | bytes 25165832 | tf_op jit(solution)/shard_map/ppermute | solution.py:68
  431.5 433.3 %collective-permute-start = (f32[512,4096]{1,0:T(8,128)}, f32[512,4096]{1,0:T(8,128)}, u32[]{:S(2)}, u32[]{:S(2)}) collective-permute-start(f32[512,4096]{1,0:T(8,128)} %fusion.51), channel_id=1, source_target_pairs={{0,8},{8,0},{1,9},{9,1},{2,10},{10,2},{3,11},{11,3},{4,12},{12,4},... | collective-permute-start | bytes 25165832 | tf_op jit(solution)/shard_map/ppermute | solution.py:68
  461.5 402.6 %collective-permute-start.33 = (f32[2,4096]{1,0:T(2,128)S(1)}, f32[2,4096]{1,0:T(2,128)S(1)}, u32[]{:S(2)}, u32[]{:S(2)}) collective-permute-start(f32[2,4096]{1,0:T(2,128)S(1)} %add.476), channel_id=1, source_target_pairs={{0,8},{8,0},{1,9},{9,1},{2,10},{10,2},{3,11},{11,3},{4,12},{12,4},... | collective-permute-start | bytes 98312 | tf_op jit(solution)/shard_map/ppermute | solution.py:73
  1341.9 34.0 %collective-permute-start.3 = (f32[512,512]{1,0:T(8,128)S(1)}, f32[512,512]{1,0:T(8,128)}, u32[]{:S(2)}, u32[]{:S(2)}) collective-permute-start(f32[512,512]{1,0:T(8,128)S(1)} %get-tuple-element.58), channel_id=1, source_target_pairs={{0,2},{1,3},{2,0},{3,1},{4,6},{5,7},{6,4},{7,5},{8,10},{9,11},{10,... | collective-permute-start | bytes 3145736 | tf_op jit(solution)/shard_map/ppermute | solution.py:102
  1343.5 46.0 %collective-permute-start.4 = (f32[512,512]{1,0:T(8,128)S(1)}, f32[512,512]{1,0:T(8,128)}, u32[]{:S(2)}, u32[]{:S(2)}) collective-permute-start(f32[512,512]{1,0:T(8,128)S(1)} %get-tuple-element.59), channel_id=1, source_target_pairs={{0,3},{1,2},{2,1},{3,0},{4,7},{5,6},{6,5},{7,4},{8,11},{9,10},{10,... | collective-permute-start | bytes 3145736 | tf_op jit(solution)/shard_map/ppermute | solution.py:102
  1343.7 75.2 %collective-permute-start.5 = (f32[512,512]{1,0:T(8,128)}, f32[512,512]{1,0:T(8,128)}, u32[]{:S(2)}, u32[]{:S(2)}) collective-permute-start(f32[512,512]{1,0:T(8,128)} %get-tuple-element.60), channel_id=1, source_target_pairs={{0,4},{1,5},{2,6},{3,7},{4,0},{5,1},{6,2},{7,3},{8,12},{9,13},{10,... | collective-permute-start | bytes 3145736 | tf_op jit(solution)/shard_map/ppermute | solution.py:102
  1345.3 90.7 %collective-permute-start.6 = (f32[512,512]{1,0:T(8,128)}, f32[512,512]{1,0:T(8,128)}, u32[]{:S(2)}, u32[]{:S(2)}) collective-permute-start(f32[512,512]{1,0:T(8,128)} %get-tuple-element.61), channel_id=1, source_target_pairs={{0,5},{1,4},{2,7},{3,6},{4,1},{5,0},{6,3},{7,2},{8,13},{9,12},{10,... | collective-permute-start | bytes 3145736 | tf_op jit(solution)/shard_map/ppermute | solution.py:102
  1373.6 64.6 %collective-permute-start.7 = (f32[512,512]{1,0:T(8,128)}, f32[512,512]{1,0:T(8,128)}, u32[]{:S(2)}, u32[]{:S(2)}) collective-permute-start(f32[512,512]{1,0:T(8,128)} %get-tuple-element.62), channel_id=1, source_target_pairs={{0,6},{1,7},{2,4},{3,5},{4,2},{5,3},{6,0},{7,1},{8,14},{9,15},{10,... | collective-permute-start | bytes 3145736 | tf_op jit(solution)/shard_map/ppermute | solution.py:102
  1375.9 68.0 %collective-permute-start.8 = (f32[512,512]{1,0:T(8,128)}, f32[512,512]{1,0:T(8,128)}, u32[]{:S(2)}, u32[]{:S(2)}) collective-permute-start(f32[512,512]{1,0:T(8,128)} %get-tuple-element.63), channel_id=1, source_target_pairs={{0,7},{1,6},{2,5},{3,4},{4,3},{5,2},{6,1},{7,0},{8,15},{9,14},{10,... | collective-permute-start | bytes 3145736 | tf_op jit(solution)/shard_map/ppermute | solution.py:102
  1389.5 54.5 %collective-permute-start.9 = (f32[512,512]{1,0:T(8,128)}, f32[512,512]{1,0:T(8,128)}, u32[]{:S(2)}, u32[]{:S(2)}) collective-permute-start(f32[512,512]{1,0:T(8,128)} %get-tuple-element.65), channel_id=1, source_target_pairs={{0,1},{1,0},{2,3},{3,2},{4,5},{5,4},{6,7},{7,6},{8,9},{9,8},{10,11... | collective-permute-start | bytes 3145736 | tf_op jit(solution)/shard_map/ppermute | solution.py:102
  1418.9 39.1 %collective-permute-start.10 = (f32[512,512]{1,0:T(8,128)}, f32[512,512]{1,0:T(8,128)}, u32[]{:S(2)}, u32[]{:S(2)}) collective-permute-start(f32[512,512]{1,0:T(8,128)} %get-tuple-element.66), channel_id=1, source_target_pairs={{0,2},{1,3},{2,0},{3,1},{4,6},{5,7},{6,4},{7,5},{8,10},{9,11},{10,... | collective-permute-start | bytes 3145736 | tf_op jit(solution)/shard_map/ppermute | solution.py:102
  1436.0 43.6 %collective-permute-start.11 = (f32[512,512]{1,0:T(8,128)}, f32[512,512]{1,0:T(8,128)}, u32[]{:S(2)}, u32[]{:S(2)}) collective-permute-start(f32[512,512]{1,0:T(8,128)} %get-tuple-element.67), channel_id=1, source_target_pairs={{0,3},{1,2},{2,1},{3,0},{4,7},{5,6},{6,5},{7,4},{8,11},{9,10},{10,... | collective-permute-start | bytes 3145736 | tf_op jit(solution)/shard_map/ppermute | solution.py:102
  1438.2 43.7 %collective-permute-start.12 = (f32[512,512]{1,0:T(8,128)}, f32[512,512]{1,0:T(8,128)}, u32[]{:S(2)}, u32[]{:S(2)}) collective-permute-start(f32[512,512]{1,0:T(8,128)} %get-tuple-element.68), channel_id=1, source_target_pairs={{0,4},{1,5},{2,6},{3,7},{4,0},{5,1},{6,2},{7,3},{8,12},{9,13},{10,... | collective-permute-start | bytes 3145736 | tf_op jit(solution)/shard_map/ppermute | solution.py:102
  1443.9 85.4 %collective-permute-start.13 = (f32[512,512]{1,0:T(8,128)S(1)}, f32[512,512]{1,0:T(8,128)}, u32[]{:S(2)}, u32[]{:S(2)}) collective-permute-start(f32[512,512]{1,0:T(8,128)S(1)} %copy-done.11), channel_id=1, source_target_pairs={{0,5},{1,4},{2,7},{3,6},{4,1},{5,0},{6,3},{7,2},{8,13},{9,12},{10,... | collective-permute-start | bytes 3145736 | tf_op jit(solution)/shard_map/ppermute | solution.py:102
  1444.0 88.4 %collective-permute-start.14 = (f32[512,512]{1,0:T(8,128)S(1)}, f32[512,512]{1,0:T(8,128)}, u32[]{:S(2)}, u32[]{:S(2)}) collective-permute-start(f32[512,512]{1,0:T(8,128)S(1)} %copy-done.10), channel_id=1, source_target_pairs={{0,6},{1,7},{2,4},{3,5},{4,2},{5,3},{6,0},{7,1},{8,14},{9,15},{10,... | collective-permute-start | bytes 3145736 | tf_op jit(solution)/shard_map/ppermute | solution.py:102
  1458.0 79.9 %collective-permute-start.15 = (f32[512,512]{1,0:T(8,128)S(1)}, f32[512,512]{1,0:T(8,128)}, u32[]{:S(2)}, u32[]{:S(2)}) collective-permute-start(f32[512,512]{1,0:T(8,128)S(1)} %copy-done.9), channel_id=1, source_target_pairs={{0,7},{1,6},{2,5},{3,4},{4,3},{5,2},{6,1},{7,0},{8,15},{9,14},{10,... | collective-permute-start | bytes 3145736 | tf_op jit(solution)/shard_map/ppermute | solution.py:102
  1479.6 59.7 %collective-permute-start.16 = (f32[512,512]{1,0:T(8,128)}, f32[512,512]{1,0:T(8,128)}, u32[]{:S(2)}, u32[]{:S(2)}) collective-permute-start(f32[512,512]{1,0:T(8,128)} %get-tuple-element.73), channel_id=1, source_target_pairs={{0,1},{1,0},{2,3},{3,2},{4,5},{5,4},{6,7},{7,6},{8,9},{9,8},{10,11... | collective-permute-start | bytes 3145736 | tf_op jit(solution)/shard_map/ppermute | solution.py:102
  1481.9 66.0 %collective-permute-start.17 = (f32[512,512]{1,0:T(8,128)}, f32[512,512]{1,0:T(8,128)}, u32[]{:S(2)}, u32[]{:S(2)}) collective-permute-start(f32[512,512]{1,0:T(8,128)} %get-tuple-element.74), channel_id=1, source_target_pairs={{0,2},{1,3},{2,0},{3,1},{4,6},{5,7},{6,4},{7,5},{8,10},{9,11},{10,... | collective-permute-start | bytes 3145736 | tf_op jit(solution)/shard_map/ppermute | solution.py:102
  1529.4 40.1 %collective-permute-start.18 = (f32[512,512]{1,0:T(8,128)}, f32[512,512]{1,0:T(8,128)S(1)}, u32[]{:S(2)}, u32[]{:S(2)}) collective-permute-start(f32[512,512]{1,0:T(8,128)} %get-tuple-element.75), channel_id=1, source_target_pairs={{0,3},{1,2},{2,1},{3,0},{4,7},{5,6},{6,5},{7,4},{8,11},{9,10},{10,... | collective-permute-start | bytes 3145736 | tf_op jit(solution)/shard_map/ppermute | solution.py:102
  1532.4 39.3 %collective-permute-start.19 = (f32[512,512]{1,0:T(8,128)S(1)}, f32[512,512]{1,0:T(8,128)S(1)}, u32[]{:S(2)}, u32[]{:S(2)}) collective-permute-start(f32[512,512]{1,0:T(8,128)S(1)} %copy-done.15), channel_id=1, source_target_pairs={{0,4},{1,5},{2,6},{3,7},{4,0},{5,1},{6,2},{7,3},{8,12},{9,13},{10,... | collective-permute-start | bytes 3145736 | tf_op jit(solution)/shard_map/ppermute | solution.py:102
  1537.9 85.5 %collective-permute-start.20 = (f32[512,512]{1,0:T(8,128)S(1)}, f32[512,512]{1,0:T(8,128)S(1)}, u32[]{:S(2)}, u32[]{:S(2)}) collective-permute-start(f32[512,512]{1,0:T(8,128)S(1)} %copy-done.14), channel_id=1, source_target_pairs={{0,5},{1,4},{2,7},{3,6},{4,1},{5,0},{6,3},{7,2},{8,13},{9,12},{10,... | collective-permute-start | bytes 3145736 | tf_op jit(solution)/shard_map/ppermute | solution.py:102
  1539.3 85.9 %collective-permute-start.21 = (f32[512,512]{1,0:T(8,128)S(1)}, f32[512,512]{1,0:T(8,128)S(1)}, u32[]{:S(2)}, u32[]{:S(2)}) collective-permute-start(f32[512,512]{1,0:T(8,128)S(1)} %copy-done.13), channel_id=1, source_target_pairs={{0,6},{1,7},{2,4},{3,5},{4,2},{5,3},{6,0},{7,1},{8,14},{9,15},{10,... | collective-permute-start | bytes 3145736 | tf_op jit(solution)/shard_map/ppermute | solution.py:102
  1547.9 78.7 %collective-permute-start.22 = (f32[512,512]{1,0:T(8,128)S(1)}, f32[512,512]{1,0:T(8,128)}, u32[]{:S(2)}, u32[]{:S(2)}) collective-permute-start(f32[512,512]{1,0:T(8,128)S(1)} %copy-done.12), channel_id=1, source_target_pairs={{0,7},{1,6},{2,5},{3,4},{4,3},{5,2},{6,1},{7,0},{8,15},{9,14},{10,... | collective-permute-start | bytes 3145736 | tf_op jit(solution)/shard_map/ppermute | solution.py:102
  1569.5 57.3 %collective-permute-start.23 = (f32[512,512]{1,0:T(8,128)S(1)}, f32[512,512]{1,0:T(8,128)}, u32[]{:S(2)}, u32[]{:S(2)}) collective-permute-start(f32[512,512]{1,0:T(8,128)S(1)} %get-tuple-element.81), channel_id=1, source_target_pairs={{0,1},{1,0},{2,3},{3,2},{4,5},{5,4},{6,7},{7,6},{8,9},{9,8},{10,11... | collective-permute-start | bytes 3145736 | tf_op jit(solution)/shard_map/ppermute | solution.py:102
  1571.7 66.0 %collective-permute-start.24 = (f32[512,512]{1,0:T(8,128)S(1)}, f32[512,512]{1,0:T(8,128)S(1)}, u32[]{:S(2)}, u32[]{:S(2)}) collective-permute-start(f32[512,512]{1,0:T(8,128)S(1)} %get-tuple-element.82), channel_id=1, source_target_pairs={{0,2},{1,3},{2,0},{3,1},{4,6},{5,7},{6,4},{7,5},{8,10},{9,11},{10,... | collective-permute-start | bytes 3145736 | tf_op jit(solution)/shard_map/ppermute | solution.py:102
  1623.4 35.9 %collective-permute-start.25 = (f32[512,512]{1,0:T(8,128)S(1)}, f32[512,512]{1,0:T(8,128)S(1)}, u32[]{:S(2)}, u32[]{:S(2)}) collective-permute-start(f32[512,512]{1,0:T(8,128)S(1)} %get-tuple-element.83), channel_id=1, source_target_pairs={{0,3},{1,2},{2,1},{3,0},{4,7},{5,6},{6,5},{7,4},{8,11},{9,10},{10,... | collective-permute-start | bytes 3145736 | tf_op jit(solution)/shard_map/ppermute | solution.py:102
  1625.2 34.2 %collective-permute-start.26 = (f32[512,512]{1,0:T(8,128)S(1)}, f32[512,512]{1,0:T(8,128)S(1)}, u32[]{:S(2)}, u32[]{:S(2)}) collective-permute-start(f32[512,512]{1,0:T(8,128)S(1)} %get-tuple-element.84), channel_id=1, source_target_pairs={{0,4},{1,5},{2,6},{3,7},{4,0},{5,1},{6,2},{7,3},{8,12},{9,13},{10,... | collective-permute-start | bytes 3145736 | tf_op jit(solution)/shard_map/ppermute | solution.py:102
  1626.7 89.5 %collective-permute-start.27 = (f32[512,512]{1,0:T(8,128)S(1)}, f32[512,512]{1,0:T(8,128)S(1)}, u32[]{:S(2)}, u32[]{:S(2)}) collective-permute-start(f32[512,512]{1,0:T(8,128)S(1)} %get-tuple-element.85), channel_id=1, source_target_pairs={{0,5},{1,4},{2,7},{3,6},{4,1},{5,0},{6,3},{7,2},{8,13},{9,12},{10,... | collective-permute-start | bytes 3145736 | tf_op jit(solution)/shard_map/ppermute | solution.py:102
  1626.8 89.4 %collective-permute-start.28 = (f32[512,512]{1,0:T(8,128)S(1)}, f32[512,512]{1,0:T(8,128)S(1)}, u32[]{:S(2)}, u32[]{:S(2)}) collective-permute-start(f32[512,512]{1,0:T(8,128)S(1)} %get-tuple-element.86), channel_id=1, source_target_pairs={{0,6},{1,7},{2,4},{3,5},{4,2},{5,3},{6,0},{7,1},{8,14},{9,15},{10,... | collective-permute-start | bytes 3145736 | tf_op jit(solution)/shard_map/ppermute | solution.py:102
  1637.8 78.6 %collective-permute-start.29 = (f32[512,512]{1,0:T(8,128)S(1)}, f32[512,512]{1,0:T(8,128)S(1)}, u32[]{:S(2)}, u32[]{:S(2)}) collective-permute-start(f32[512,512]{1,0:T(8,128)S(1)} %get-tuple-element.87), channel_id=1, source_target_pairs={{0,7},{1,6},{2,5},{3,4},{4,3},{5,2},{6,1},{7,0},{8,15},{9,14},{10,... | collective-permute-start | bytes 3145736 | tf_op jit(solution)/shard_map/ppermute | solution.py:102
  (49 other events, 1599.6 us)
Sparse Core Ops, SparseCore 0:
  25.2 246.5 all-gather.4
  274.1 398.1 all-gather.6

commit v3 on v2

--- a/solution.py
+++ b/solution.py
@@ -6,7 +6,8 @@
 
 NORM_EPS = 1e-6
 MTP_LAMBDA = 0.3
-CHUNKS = 4
+UNIT = 256
+CHUNKS = (2, 2, 2, 2)
 
 
 def solution(mesh):
@@ -22,13 +23,16 @@
         tp_rank = lax.axis_index('tp')
         gains = (gain_final[None, :], gain_mtp[None, :])
 
-        normed, gathered = [], []
+        def normalise(h):
+            x = h.reshape(-1, d_model).astype(jnp.float32)
+            inv = lax.rsqrt(jnp.mean(x * x, axis=-1, keepdims=True) + NORM_EPS)
+            return x * inv, inv
+
+        gathered = []
         for h in (h_main, h_mtp):
-            x = h.reshape(rows, d_model).astype(jnp.float32)
-            inv = lax.rsqrt(jnp.mean(x * x, axis=-1, keepdims=True) + NORM_EPS)
-            n = x * inv
-            normed.append(n)
-            gathered.append(lax.all_gather(lax.dynamic_slice_in_dim(n, tp_rank * half, half, 0), ('tp', 'dp'), axis=0, tiled=True))
+            h_half = lax.optimization_barrier(lax.dynamic_slice_in_dim(h.reshape(rows, d_model), tp_rank * half, half, 0))
+            gathered.append(lax.all_gather(normalise(h_half)[0], ('tp', 'dp'), axis=0, tiled=True))
+        normed = [normalise(h)[0] for h in (h_main, h_mtp)]
 
         vocab_start = tp_rank * shard_vocab
         column = jnp.arange(shard_vocab, dtype=jnp.int32)[None, :]
@@ -63,8 +67,7 @@
         for which in range(2):
             part = lax.dot_general(grad_z[which * rows:(which + 1) * rows], w_out, (((1,), (1,)), ((), ())), preferred_element_type=jnp.float32).astype(jnp.bfloat16).astype(jnp.float32)
             h, part = lax.optimization_barrier(((h_main, h_mtp)[which], part))
-            x = h.reshape(rows, d_model).astype(jnp.float32)
-            gain_parts.append(jnp.sum(part * (x * lax.rsqrt(jnp.mean(x * x, axis=-1, keepdims=True) + NORM_EPS)), axis=0))
+            gain_parts.append(jnp.sum(part * normalise(h)[0], axis=0))
             grad_u.append((part, lax.ppermute(part, 'tp', [(i, n_tp - 1 - i) for i in range(n_tp)])))
         grad_gain = jnp.stack(gain_parts)
         for axis, size in (('dp', n_dp), ('tp', n_tp)):
@@ -73,10 +76,15 @@
                 grad_gain = grad_gain + lax.ppermute(grad_gain, axis, [(i, i ^ bit) for i in range(size)])
                 bit *= 2
 
-        width = -(-shard_vocab // (n_dp * 256)) * 256
-        col_unit = jnp.minimum(dp_rank * (width // 256), (shard_vocab - width) // 256)
-        w_slice = lax.dynamic_slice_in_dim(w_out, col_unit * 256, width, 1)
-        slice_start = vocab_start + col_unit * 256
+        units = sum(CHUNKS)
+        width = units * UNIT
+        assert n_dp * width >= shard_vocab and shard_vocab % UNIT == 0
+
+        def first_unit(rank):
+            return jnp.minimum(rank * units, shard_vocab // UNIT - units)
+
+        w_slice = lax.dynamic_slice_in_dim(w_out, first_unit(dp_rank) * UNIT, width, 1)
+        slice_start = vocab_start + first_unit(dp_rank) * UNIT
 
         def token_order(a):
             return a.reshape(n_dp, n_tp, half).transpose(1, 0, 2).reshape(n_dp * rows)
@@ -91,29 +99,28 @@
         u_all = [(n * g).astype(jnp.bfloat16) for n, g in zip(gathered, gains)]
         d_loc = d_model // n_dp
         grad_w = jnp.zeros((d_loc, shard_vocab), jnp.float32)
-        cw = width // CHUNKS
-        for q in range(CHUNKS):
-            cols = w_slice[:, q * cw:(q + 1) * cw]
-            part = slice_grad(0, u_all[0], cols, slice_start + q * cw)
-            part = part + slice_grad(1, u_all[1], cols, slice_start + q * cw)
+        grad_main = slice_grad(0, u_all[0], w_slice, slice_start)
+        for q, chunk in enumerate(CHUNKS):
+            done = sum(CHUNKS[:q])
+            lo, cw = done * UNIT, chunk * UNIT
+            cols = w_slice[:, lo:lo + cw]
+            part = grad_main[:, lo:lo + cw] + slice_grad(1, u_all[1], cols, slice_start + lo)
             sends = lax.optimization_barrier([lax.dynamic_slice(part, ((dp_rank ^ k) * d_loc, 0), (d_loc, cw)) for k in range(n_dp)])
             for k, block in enumerate(sends):
                 if k:
                     block = lax.ppermute(block, 'dp', [(i, i ^ k) for i in range(n_dp)])
-                peer_unit = jnp.minimum((dp_rank ^ k) * (width // 256), (shard_vocab - width) // 256)
-                grad_w = lax.dynamic_update_slice(grad_w, block, (0, (peer_unit + q * cw // 256) * 256))
+                grad_w = lax.dynamic_update_slice(grad_w, block, (0, (first_unit(dp_rank ^ k) + done) * UNIT))
 
         grads_h = []
         for which, h in enumerate((h_main, h_mtp)):
             h, part, other = lax.optimization_barrier((h, *grad_u[which]))
-            x = h.reshape(rows, d_model).astype(jnp.float32)
-            inv = lax.rsqrt(jnp.mean(x * x, axis=-1, keepdims=True) + NORM_EPS)
-            n = x * inv
+            n, inv = normalise(h)
             du = part + other
             grad_normed = du * gains[which]
             grad_x = inv * (grad_normed - n * jnp.mean(grad_normed * n, axis=-1, keepdims=True))
             grads_h.append(grad_x.astype(jnp.bfloat16).reshape(batch_loc, seq_len, d_model))
         return loss_total, grads_h[0], grads_h[1], grad_w, grad_gain[0], grad_gain[1]
 
+
     row_spec = P('dp', None)
     return jax.shard_map(layer_step, mesh=mesh, in_specs=(P('dp', None, None), P('dp', None, None), row_spec, row_spec, row_spec, row_spec, P(None), P(None), P(None, 'tp')), out_specs=(P(), P('dp', None, None), P('dp', None, None), P('dp', 'tp'), P(None), P(None)), check_vma=False)

time: 1740 us -> 1660 us (0.954)
  matrix products: 740 us -> 699 us
  other arithmetic: 192 us -> 160 us
    convert_element_type x2 -> x1, other arithmetic: 65.4 us -> 32.7 us  [layer_step(): u_all = [(n * g).astype(jnp.bfloat16) for n, g in zip(gathered, gains)]]
    dot_general x8 -> x5, matrix products: 210 us -> 190 us  [slice_grad(): z = jnp.dot(u_all, cols, preferred_element_type=jnp.float32)]
    dot_general x8 -> x5, matrix products: 211 us -> 196 us  [slice_grad(): lax.dot_general(u_all, e, (((0,), (0,)), ((), ())), preferred_element_typ...]
  transfers between devices with their start and end apart: 36 -> 36, of which waited for: 14 -> 14; matrix products, arithmetic and copies ran while one was open for 35% -> 36% of each run, Pallas kernels for 0% -> 0%
where the time goes in v3:
time: 1660 us
  matrix products  699 us (42%)
  waiting for transfers between devices  659 us (40%)
  other arithmetic  160 us (10%)
  local copies, waits for them, and re-layouts  68.5 us (4%)
  starting transfers between devices  36.1 us (2%)
  blocking collectives  17 us (1%)
    ppermute x4, waiting for transfers between devices, layer_step(): lax.ppermute(grad_gain, axis, [(i, i ^ bit) for i in range(size)])  406 us
    ppermute x28, waiting for transfers between devices, layer_step(): block = lax.ppermute(block, 'dp', [(i, i ^ k) for i in range(n_dp)])  253 us
    dot_general x5, matrix products, slice_grad(): lax.dot_general(u_all, e, (((0,), (0,)), ((), ())), preferred_element_typ...  196 us
    dot_general x5, matrix products, slice_grad(): z = jnp.dot(u_all, cols, preferred_element_type=jnp.float32)  190 us
    dot_general x2, matrix products, layer_step(): lax.dot_general(grad_z[which * rows:(which + 1) * rows], w_out, (((1,), (...  165 us
    dot_general x1, matrix products, layer_step(): logits = jnp.dot(u_rows, w_out, preferred_element_type=jnp.float32)  149 us
    convert_element_type x1, other arithmetic, layer_step(): (own_row_w[:, None] * jnp.where(is_target, probs - 1.0, probs)).astype(jn...  34.7 us
  transfers between devices with their start and end apart: 36, of which 14 were waited for; matrix products, arithmetic and copies ran while one was open for 36% of the time, Pallas kernels for 0%

profile of v3, /device:TPU:0, one launch (start us, length us, event | category | flops | bytes accessed | tf_op | source)
XLA Modules:
  0.0 1655.8 jit_solution(9307519933513367181)
XLA Ops:
  30.3 148.5 %fusion.84 = (f32[1024]{0:T(1024)S(1)}, f32[1024,16128]{1,0:T(8,128)}) fusion(bf16[4096,16128]{1,0:T(8,128)(2,1)} %param.18, bf16[512,4096]{1,0:T(8,128)(2,1)S(1)} %fusion.27, bf16[512,4096]{1,0:T(8,128)(2,1)S(1)} %fusion.24), kind=kOutput, calls=%fused_computation.211 | convolution fusion | flops 135324762112 | bytes 206573568 | tf_op jit(solution)/shard_map/dot_general | solution.py:44
  178.9 24.7 %select_reduce_fusion = (f32[1024]{0:T(1024)S(1)}, f32[1024]{0:T(1024)S(1)}) fusion(f32[1024,16128]{1,0:T(8,128)} %get-tuple-element.138, s32[1024]{0:T(1024)S(1)} %copy-done.29, f32[1024]{0:T(1024)S(1)} %get-tuple-element.137), kind=kLoop, calls=%fused_computation.5 | loop fusion | flops 82573312 | bytes 66076672 | tf_op jit(solution)/shard_map/reduce_sum | solution.py:48
  203.6 17.0 %all-gather.1 = f32[16,5,1024]{2,1,0:T(8,128)S(1)} all-gather(f32[1,5,1024]{2,1,0:T(8,128)S(1)} %bitcast.148), channel_id=2, replica_groups=mesh['tp'=2,'dp'=8] {'tp','dp'}, dimensions={0}, use_global_device_ids=true | all-gather | bytes 348160 | tf_op jit(solution)/shard_map/all_gather | solution.py:51
  222.5 34.7 %fusion.1 = bf16[1024,16128]{1,0:T(8,128)(2,1)} fusion(f32[1024,16128]{1,0:T(8,128)} %get-tuple-element.138, f32[1024]{0:T(1024)S(1)} %bitcast.156, f32[1024]{0:T(1024)S(1)} %bitcast.155, s32[1024]{0:T(1024)S(1)} %copy-done.29), kind=kLoop, calls=%fused_computation.4 | loop fusion | flops 99090432 | bytes 99102720 | tf_op jit(solution)/shard_map/convert_element_type | solution.py:65
  257.2 82.6 %fusion.57 = f32[512,4096]{1,0:T(8,128)} fusion(bf16[4096,16128]{1,0:T(8,128)(2,1)} %param.18, bf16[1024,16128]{1,0:T(8,128)(2,1)} %fusion.1), kind=kOutput, calls=%fused_computation.80 | convolution fusion | flops 67649929216 | bytes 157024256 | tf_op jit(solution)/shard_map/dot_general | solution.py:68
  341.4 82.3 %fusion.51 = f32[512,4096]{1,0:T(8,128)} fusion(bf16[4096,16128]{1,0:T(8,128)(2,1)} %param.18, bf16[1024,16128]{1,0:T(8,128)(2,1)} %fusion.1), kind=kOutput, calls=%fused_computation.78 | convolution fusion | flops 67649929216 | bytes 157024256 | tf_op jit(solution)/shard_map/dot_general | solution.py:68
  452.2 398.9 %collective-permute-done.33 = f32[2,4096]{1,0:T(2,128)S(1)} collective-permute-done((f32[2,4096]{1,0:T(2,128)S(1)}, f32[2,4096]{1,0:T(2,128)S(1)}, u32[]{:S(2)}, u32[]{:S(2)}) %collective-permute-start.33) | collective-permute-done | bytes 32800 | tf_op jit(solution)/shard_map/ppermute | solution.py:76
  854.9 8.2 fusion.14
  871.8 6.6 fusion.63
  878.5 6.9 fusion.62
  885.3 32.7 %multiply_convert_fusion = bf16[4096,4096]{1,0:T(8,128)(2,1)} fusion(f32[4096,4096]{1,0:T(8,128)} %all-gather.7.cloned.1.call-done, f32[4096]{0:T(1024)S(1)} %copy-done.22), kind=kLoop, calls=%fused_computation.1 | loop fusion | flops 33554432 | bytes 100679680 | tf_op jit(solution)/shard_map/convert_element_type | solution.py:99
  918.0 26.2 %fusion.43 = bf16[4096,512]{1,0:T(8,128)(2,1)} fusion(bf16[4096,4096]{1,0:T(8,128)(2,1)} %multiply_convert_fusion, bf16[4096,16128]{1,0:T(8,128)(2,1)} %param.18, s32[]{:T(128)S(6)} %add.505, s32[512]{0:T(512)S(1)} %iota_add_fusion.1, f32[4096]{0:T(1024)S(1)} %bitcast.164, f32[4096]{0:T(1024)S(1)} %bitcast.160, s32[4096]{0:T(1024)S(1)} %bitcast.168), kind=kOutput, calls=%fused_computation.66 | convolution fusion | flops 17192452096 | bytes 41994244 | tf_op jit(solution)/shard_map/dot_general | solution.py:93
  944.3 84.9 %fusion.3 = bf16[4096,2048]{1,0:T(8,128)(2,1)} fusion(f32[4096]{0:T(1024)S(1)} %bitcast.173, bf16[4096,16128]{1,0:T(8,128)(2,1)} %param.18, s32[]{:T(128)S(6)} %select_n.183, s32[2048]{0:T(1024)S(1)} %iota_add_fusion, f32[4096]{0:T(1024)S(1)} %bitcast.172, s32[4096]{0:T(1024)S(1)} %bitcast.174, f32[4096,4096]{1,0:T(8,128)} %all-gather.5.cloned.1.call-done, ...), kind=kOutput, calls=%fused_computation.10 | convolution fusion | flops 68803362816 | bytes 100737024 | tf_op jit(solution)/shard_map/dot_general | solution.py:93
  1029.2 82.4 %fusion.9 = f32[4096,2048]{1,0:T(8,128)} fusion(bf16[4096,2048]{1,0:T(8,128)(2,1)} %fusion.3, f32[4096,4096]{1,0:T(8,128)} %all-gather.5.cloned.1.call-done, f32[4096]{0:T(1024)S(1)} %copy-done.28), kind=kOutput, calls=%fused_computation.16 | convolution fusion | flops 68753031168 | bytes 117456896 | tf_op jit(solution)/shard_map/dot_general | solution.py:97
  1111.6 28.3 %slice_add_fusion = f32[4096,512]{1,0:T(8,128)} fusion(f32[4096,2048]{1,0:T(8,128)} %fusion.9, bf16[4096,4096]{1,0:T(8,128)(2,1)} %multiply_convert_fusion, bf16[4096,512]{1,0:T(8,128)(2,1)} %fusion.43), kind=kOutput, calls=%fused_computation.67 | convolution fusion | flops 17181966336 | bytes 54525952 | tf_op jit(solution)/shard_map/dot_general | solution.py:97
  1140.0 26.4 %fusion.39 = bf16[4096,512]{1,0:T(8,128)(2,1)} fusion(bf16[4096,4096]{1,0:T(8,128)(2,1)} %multiply_convert_fusion, bf16[4096,16128]{1,0:T(8,128)(2,1)} %param.18, s32[]{:T(128)S(6)} %add.503, s32[512]{0:T(512)S(1)} %copy-done.42, f32[4096]{0:T(1024)S(1)} %bitcast.165, f32[4096]{0:T(1024)S(1)} %bitcast.161, s32[4096]{0:T(1024)S(1)} %bitcast.169), kind=kOutput, calls=%fused_computation.62 | convolution fusion | flops 17192452096 | bytes 41994244 | tf_op jit(solution)/shard_map/dot_general | solution.py:93
  1166.4 28.3 %slice_add_fusion.2 = f32[4096,512]{1,0:T(8,128)} fusion(f32[4096,2048]{1,0:T(8,128)} %fusion.9, bf16[4096,4096]{1,0:T(8,128)(2,1)} %multiply_convert_fusion, bf16[4096,512]{1,0:T(8,128)(2,1)} %fusion.39), kind=kOutput, calls=%fused_computation.69 | convolution fusion | flops 17181966336 | bytes 54525952 | tf_op jit(solution)/shard_map/dot_general | solution.py:97
  1194.7 6.9 constant_dynamic-slice_fusion.16
  1201.6 26.6 %fusion.37 = bf16[4096,512]{1,0:T(8,128)(2,1)} fusion(bf16[4096,4096]{1,0:T(8,128)(2,1)} %multiply_convert_fusion, bf16[4096,16128]{1,0:T(8,128)(2,1)} %param.18, s32[]{:T(128)S(6)} %select_n.183, f32[4096]{0:T(1024)S(1)} %bitcast.166, s32[512]{0:T(512)S(1)} %copy-done.41, f32[4096]{0:T(1024)S(1)} %bitcast.162, s32[4096]{0:T(1024)S(1)} %bitcast.170), kind=kOutput, calls=%fused_computation.60 | convolution fusion | flops 17192452096 | bytes 41994244 | tf_op jit(solution)/shard_map/dot_general | solution.py:93
  1228.2 28.2 %slice_add_fusion.3 = f32[4096,512]{1,0:T(8,128)} fusion(f32[4096,2048]{1,0:T(8,128)} %fusion.9, bf16[4096,4096]{1,0:T(8,128)(2,1)} %multiply_convert_fusion, bf16[4096,512]{1,0:T(8,128)(2,1)} %fusion.37), kind=kOutput, calls=%fused_computation.70 | convolution fusion | flops 17181966336 | bytes 54525952 | tf_op jit(solution)/shard_map/dot_general | solution.py:97
  1265.9 26.3 %fusion.41 = bf16[4096,512]{1,0:T(8,128)(2,1)} fusion(bf16[4096,4096]{1,0:T(8,128)(2,1)} %multiply_convert_fusion, bf16[4096,16128]{1,0:T(8,128)(2,1)} %param.18, s32[]{:T(128)S(6)} %add.504, s32[512]{0:T(512)S(1)} %copy-done.40, f32[4096]{0:T(1024)S(1)} %bitcast.167, f32[4096]{0:T(1024)S(1)} %bitcast.163, s32[4096]{0:T(1024)S(1)} %bitcast.171), kind=kOutput, calls=%fused_computation.64 | convolution fusion | flops 17192452096 | bytes 41994244 | tf_op jit(solution)/shard_map/dot_general | solution.py:93
  1295.0 15.0 collective-permute-done.4
  1312.2 28.3 %slice_add_fusion.1 = f32[4096,512]{1,0:T(8,128)} fusion(f32[4096,2048]{1,0:T(8,128)} %fusion.9, bf16[4096,4096]{1,0:T(8,128)(2,1)} %multiply_convert_fusion, bf16[4096,512]{1,0:T(8,128)(2,1)} %fusion.41), kind=kOutput, calls=%fused_computation.68 | convolution fusion | flops 17181966336 | bytes 54525952 | tf_op jit(solution)/shard_map/dot_general | solution.py:97
  1341.9 14.5 collective-permute-done.6
  1381.0 19.1 %collective-permute-done.11 = f32[512,512]{1,0:T(8,128)} collective-permute-done((f32[512,512]{1,0:T(8,128)}, f32[512,512]{1,0:T(8,128)}, u32[]{:S(2)}, u32[]{:S(2)}) %collective-permute-start.11) | collective-permute-done | bytes 1048608 | tf_op jit(solution)/shard_map/ppermute | solution.py:111
  1405.2 44.8 %collective-permute-done.13 = f32[512,512]{1,0:T(8,128)} collective-permute-done((f32[512,512]{1,0:T(8,128)S(1)}, f32[512,512]{1,0:T(8,128)}, u32[]{:S(2)}, u32[]{:S(2)}) %collective-permute-start.13) | collective-permute-done | bytes 1048608 | tf_op jit(solution)/shard_map/ppermute | solution.py:111
  1470.9 19.0 %collective-permute-done.18 = f32[512,512]{1,0:T(8,128)S(1)} collective-permute-done((f32[512,512]{1,0:T(8,128)}, f32[512,512]{1,0:T(8,128)S(1)}, u32[]{:S(2)}, u32[]{:S(2)}) %collective-permute-start.18) | collective-permute-done | bytes 1048608 | tf_op jit(solution)/shard_map/ppermute | solution.py:111
  1497.7 46.3 %collective-permute-done.20 = f32[512,512]{1,0:T(8,128)S(1)} collective-permute-done((f32[512,512]{1,0:T(8,128)S(1)}, f32[512,512]{1,0:T(8,128)S(1)}, u32[]{:S(2)}, u32[]{:S(2)}) %collective-permute-start.20) | collective-permute-done | bytes 1048608 | tf_op jit(solution)/shard_map/ppermute | solution.py:111
  1548.6 9.7 collective-permute-done.24
  1562.2 17.6 %collective-permute-done.25 = f32[512,512]{1,0:T(8,128)S(1)} collective-permute-done((f32[512,512]{1,0:T(8,128)S(1)}, f32[512,512]{1,0:T(8,128)S(1)}, u32[]{:S(2)}, u32[]{:S(2)}) %collective-permute-start.25) | collective-permute-done | bytes 1048608 | tf_op jit(solution)/shard_map/ppermute | solution.py:111
  1580.0 56.7 %collective-permute-done.27 = f32[512,512]{1,0:T(8,128)S(1)} collective-permute-done((f32[512,512]{1,0:T(8,128)S(1)}, f32[512,512]{1,0:T(8,128)S(1)}, u32[]{:S(2)}, u32[]{:S(2)}) %collective-permute-start.27) | collective-permute-done | bytes 1048608 | tf_op jit(solution)/shard_map/ppermute | solution.py:111
  1637.0 11.5 copy-done.7
  (261 shorter events, 150.1 us)
Async XLA Ops:
  7.2 878.2 %all-gather.7.cloned.1.call-start = ((), (), s32[]{:S(2)}) async-start(), calls=%async_computation.1 | async-start | bytes 71303168 | tf_op jit(solution)/shard_map/all_gather | solution.py:34
  12.1 932.2 %all-gather.5.cloned.1.call-start = ((), (), s32[]{:S(2)}) async-start(), calls=%async_computation | async-start | bytes 71303168 | tf_op jit(solution)/shard_map/all_gather | solution.py:34
  339.8 512.0 %collective-permute-start.1 = (f32[512,4096]{1,0:T(8,128)}, f32[512,4096]{1,0:T(8,128)}, u32[]{:S(2)}, u32[]{:S(2)}) collective-permute-start(f32[512,4096]{1,0:T(8,128)} %fusion.57), channel_id=1, source_target_pairs={{0,8},{8,0},{1,9},{9,1},{2,10},{10,2},{3,11},{11,3},{4,12},{12,4},... | collective-permute-start | bytes 25165832 | tf_op jit(solution)/shard_map/ppermute | solution.py:71
  423.7 428.1 %collective-permute-start = (f32[512,4096]{1,0:T(8,128)}, f32[512,4096]{1,0:T(8,128)}, u32[]{:S(2)}, u32[]{:S(2)}) collective-permute-start(f32[512,4096]{1,0:T(8,128)} %fusion.51), channel_id=1, source_target_pairs={{0,8},{8,0},{1,9},{9,1},{2,10},{10,2},{3,11},{11,3},{4,12},{12,4},... | collective-permute-start | bytes 25165832 | tf_op jit(solution)/shard_map/ppermute | solution.py:71
  449.6 401.5 %collective-permute-start.33 = (f32[2,4096]{1,0:T(2,128)S(1)}, f32[2,4096]{1,0:T(2,128)S(1)}, u32[]{:S(2)}, u32[]{:S(2)}) collective-permute-start(f32[2,4096]{1,0:T(2,128)S(1)} %add.493), channel_id=1, source_target_pairs={{0,8},{8,0},{1,9},{9,1},{2,10},{10,2},{3,11},{11,3},{4,12},{12,4},... | collective-permute-start | bytes 98312 | tf_op jit(solution)/shard_map/ppermute | solution.py:76
  1262.5 32.2 %collective-permute-start.3 = (f32[512,512]{1,0:T(8,128)S(1)}, f32[512,512]{1,0:T(8,128)S(1)}, u32[]{:S(2)}, u32[]{:S(2)}) collective-permute-start(f32[512,512]{1,0:T(8,128)S(1)} %get-tuple-element.58), channel_id=1, source_target_pairs={{0,2},{1,3},{2,0},{3,1},{4,6},{5,7},{6,4},{7,5},{8,10},{9,11},{10,... | collective-permute-start | bytes 3145736 | tf_op jit(solution)/shard_map/ppermute | solution.py:111
  1263.9 46.1 %collective-permute-start.4 = (f32[512,512]{1,0:T(8,128)S(1)}, f32[512,512]{1,0:T(8,128)S(1)}, u32[]{:S(2)}, u32[]{:S(2)}) collective-permute-start(f32[512,512]{1,0:T(8,128)S(1)} %get-tuple-element.59), channel_id=1, source_target_pairs={{0,3},{1,2},{2,1},{3,0},{4,7},{5,6},{6,5},{7,4},{8,11},{9,10},{10,... | collective-permute-start | bytes 3145736 | tf_op jit(solution)/shard_map/ppermute | solution.py:111
  1264.3 76.2 %collective-permute-start.5 = (f32[512,512]{1,0:T(8,128)}, f32[512,512]{1,0:T(8,128)}, u32[]{:S(2)}, u32[]{:S(2)}) collective-permute-start(f32[512,512]{1,0:T(8,128)} %get-tuple-element.60), channel_id=1, source_target_pairs={{0,4},{1,5},{2,6},{3,7},{4,0},{5,1},{6,2},{7,3},{8,12},{9,13},{10,... | collective-permute-start | bytes 3145736 | tf_op jit(solution)/shard_map/ppermute | solution.py:111
  1265.9 90.6 %collective-permute-start.6 = (f32[512,512]{1,0:T(8,128)}, f32[512,512]{1,0:T(8,128)}, u32[]{:S(2)}, u32[]{:S(2)}) collective-permute-start(f32[512,512]{1,0:T(8,128)} %get-tuple-element.61), channel_id=1, source_target_pairs={{0,5},{1,4},{2,7},{3,6},{4,1},{5,0},{6,3},{7,2},{8,13},{9,12},{10,... | collective-permute-start | bytes 3145736 | tf_op jit(solution)/shard_map/ppermute | solution.py:111
  1292.2 66.3 %collective-permute-start.7 = (f32[512,512]{1,0:T(8,128)}, f32[512,512]{1,0:T(8,128)}, u32[]{:S(2)}, u32[]{:S(2)}) collective-permute-start(f32[512,512]{1,0:T(8,128)} %get-tuple-element.62), channel_id=1, source_target_pairs={{0,6},{1,7},{2,4},{3,5},{4,2},{5,3},{6,0},{7,1},{8,14},{9,15},{10,... | collective-permute-start | bytes 3145736 | tf_op jit(solution)/shard_map/ppermute | solution.py:111
  1294.6 69.9 %collective-permute-start.8 = (f32[512,512]{1,0:T(8,128)}, f32[512,512]{1,0:T(8,128)}, u32[]{:S(2)}, u32[]{:S(2)}) collective-permute-start(f32[512,512]{1,0:T(8,128)} %get-tuple-element.63), channel_id=1, source_target_pairs={{0,7},{1,6},{2,5},{3,4},{4,3},{5,2},{6,1},{7,0},{8,15},{9,14},{10,... | collective-permute-start | bytes 3145736 | tf_op jit(solution)/shard_map/ppermute | solution.py:111
  1311.0 53.6 %collective-permute-start.9 = (f32[512,512]{1,0:T(8,128)}, f32[512,512]{1,0:T(8,128)}, u32[]{:S(2)}, u32[]{:S(2)}) collective-permute-start(f32[512,512]{1,0:T(8,128)} %get-tuple-element.65), channel_id=1, source_target_pairs={{0,1},{1,0},{2,3},{3,2},{4,5},{5,4},{6,7},{7,6},{8,9},{9,8},{10,11... | collective-permute-start | bytes 3145736 | tf_op jit(solution)/shard_map/ppermute | solution.py:111
  1340.5 38.0 %collective-permute-start.10 = (f32[512,512]{1,0:T(8,128)}, f32[512,512]{1,0:T(8,128)}, u32[]{:S(2)}, u32[]{:S(2)}) collective-permute-start(f32[512,512]{1,0:T(8,128)} %get-tuple-element.66), channel_id=1, source_target_pairs={{0,2},{1,3},{2,0},{3,1},{4,6},{5,7},{6,4},{7,5},{8,10},{9,11},{10,... | collective-permute-start | bytes 3145736 | tf_op jit(solution)/shard_map/ppermute | solution.py:111
  1356.5 43.6 %collective-permute-start.11 = (f32[512,512]{1,0:T(8,128)}, f32[512,512]{1,0:T(8,128)}, u32[]{:S(2)}, u32[]{:S(2)}) collective-permute-start(f32[512,512]{1,0:T(8,128)} %get-tuple-element.67), channel_id=1, source_target_pairs={{0,3},{1,2},{2,1},{3,0},{4,7},{5,6},{6,5},{7,4},{8,11},{9,10},{10,... | collective-permute-start | bytes 3145736 | tf_op jit(solution)/shard_map/ppermute | solution.py:111
  1358.5 43.9 %collective-permute-start.12 = (f32[512,512]{1,0:T(8,128)}, f32[512,512]{1,0:T(8,128)}, u32[]{:S(2)}, u32[]{:S(2)}) collective-permute-start(f32[512,512]{1,0:T(8,128)} %get-tuple-element.68), channel_id=1, source_target_pairs={{0,4},{1,5},{2,6},{3,7},{4,0},{5,1},{6,2},{7,3},{8,12},{9,13},{10,... | collective-permute-start | bytes 3145736 | tf_op jit(solution)/shard_map/ppermute | solution.py:111
  1364.5 85.4 %collective-permute-start.13 = (f32[512,512]{1,0:T(8,128)S(1)}, f32[512,512]{1,0:T(8,128)}, u32[]{:S(2)}, u32[]{:S(2)}) collective-permute-start(f32[512,512]{1,0:T(8,128)S(1)} %copy-done.13), channel_id=1, source_target_pairs={{0,5},{1,4},{2,7},{3,6},{4,1},{5,0},{6,3},{7,2},{8,13},{9,12},{10,... | collective-permute-start | bytes 3145736 | tf_op jit(solution)/shard_map/ppermute | solution.py:111
  1364.6 88.2 %collective-permute-start.14 = (f32[512,512]{1,0:T(8,128)S(1)}, f32[512,512]{1,0:T(8,128)}, u32[]{:S(2)}, u32[]{:S(2)}) collective-permute-start(f32[512,512]{1,0:T(8,128)S(1)} %copy-done.12), channel_id=1, source_target_pairs={{0,6},{1,7},{2,4},{3,5},{4,2},{5,3},{6,0},{7,1},{8,14},{9,15},{10,... | collective-permute-start | bytes 3145736 | tf_op jit(solution)/shard_map/ppermute | solution.py:111
  1378.5 79.8 %collective-permute-start.15 = (f32[512,512]{1,0:T(8,128)S(1)}, f32[512,512]{1,0:T(8,128)}, u32[]{:S(2)}, u32[]{:S(2)}) collective-permute-start(f32[512,512]{1,0:T(8,128)S(1)} %copy-done.11), channel_id=1, source_target_pairs={{0,7},{1,6},{2,5},{3,4},{4,3},{5,2},{6,1},{7,0},{8,15},{9,14},{10,... | collective-permute-start | bytes 3145736 | tf_op jit(solution)/shard_map/ppermute | solution.py:111
  1400.1 59.6 %collective-permute-start.16 = (f32[512,512]{1,0:T(8,128)}, f32[512,512]{1,0:T(8,128)}, u32[]{:S(2)}, u32[]{:S(2)}) collective-permute-start(f32[512,512]{1,0:T(8,128)} %get-tuple-element.73), channel_id=1, source_target_pairs={{0,1},{1,0},{2,3},{3,2},{4,5},{5,4},{6,7},{7,6},{8,9},{9,8},{10,11... | collective-permute-start | bytes 3145736 | tf_op jit(solution)/shard_map/ppermute | solution.py:111
  1402.4 66.0 %collective-permute-start.17 = (f32[512,512]{1,0:T(8,128)}, f32[512,512]{1,0:T(8,128)}, u32[]{:S(2)}, u32[]{:S(2)}) collective-permute-start(f32[512,512]{1,0:T(8,128)} %get-tuple-element.74), channel_id=1, source_target_pairs={{0,2},{1,3},{2,0},{3,1},{4,6},{5,7},{6,4},{7,5},{8,10},{9,11},{10,... | collective-permute-start | bytes 3145736 | tf_op jit(solution)/shard_map/ppermute | solution.py:111
  1450.0 39.9 %collective-permute-start.18 = (f32[512,512]{1,0:T(8,128)}, f32[512,512]{1,0:T(8,128)S(1)}, u32[]{:S(2)}, u32[]{:S(2)}) collective-permute-start(f32[512,512]{1,0:T(8,128)} %get-tuple-element.75), channel_id=1, source_target_pairs={{0,3},{1,2},{2,1},{3,0},{4,7},{5,6},{6,5},{7,4},{8,11},{9,10},{10,... | collective-permute-start | bytes 3145736 | tf_op jit(solution)/shard_map/ppermute | solution.py:111
  1452.8 39.5 %collective-permute-start.19 = (f32[512,512]{1,0:T(8,128)S(1)}, f32[512,512]{1,0:T(8,128)S(1)}, u32[]{:S(2)}, u32[]{:S(2)}) collective-permute-start(f32[512,512]{1,0:T(8,128)S(1)} %copy-done.17), channel_id=1, source_target_pairs={{0,4},{1,5},{2,6},{3,7},{4,0},{5,1},{6,2},{7,3},{8,12},{9,13},{10,... | collective-permute-start | bytes 3145736 | tf_op jit(solution)/shard_map/ppermute | solution.py:111
  1458.3 85.7 %collective-permute-start.20 = (f32[512,512]{1,0:T(8,128)S(1)}, f32[512,512]{1,0:T(8,128)S(1)}, u32[]{:S(2)}, u32[]{:S(2)}) collective-permute-start(f32[512,512]{1,0:T(8,128)S(1)} %copy-done.16), channel_id=1, source_target_pairs={{0,5},{1,4},{2,7},{3,6},{4,1},{5,0},{6,3},{7,2},{8,13},{9,12},{10,... | collective-permute-start | bytes 3145736 | tf_op jit(solution)/shard_map/ppermute | solution.py:111
  1459.7 86.0 %collective-permute-start.21 = (f32[512,512]{1,0:T(8,128)S(1)}, f32[512,512]{1,0:T(8,128)S(1)}, u32[]{:S(2)}, u32[]{:S(2)}) collective-permute-start(f32[512,512]{1,0:T(8,128)S(1)} %copy-done.15), channel_id=1, source_target_pairs={{0,6},{1,7},{2,4},{3,5},{4,2},{5,3},{6,0},{7,1},{8,14},{9,15},{10,... | collective-permute-start | bytes 3145736 | tf_op jit(solution)/shard_map/ppermute | solution.py:111
  1468.5 78.7 %collective-permute-start.22 = (f32[512,512]{1,0:T(8,128)S(1)}, f32[512,512]{1,0:T(8,128)}, u32[]{:S(2)}, u32[]{:S(2)}) collective-permute-start(f32[512,512]{1,0:T(8,128)S(1)} %copy-done.14), channel_id=1, source_target_pairs={{0,7},{1,6},{2,5},{3,4},{4,3},{5,2},{6,1},{7,0},{8,15},{9,14},{10,... | collective-permute-start | bytes 3145736 | tf_op jit(solution)/shard_map/ppermute | solution.py:111
  1489.9 57.4 %collective-permute-start.23 = (f32[512,512]{1,0:T(8,128)S(1)}, f32[512,512]{1,0:T(8,128)}, u32[]{:S(2)}, u32[]{:S(2)}) collective-permute-start(f32[512,512]{1,0:T(8,128)S(1)} %get-tuple-element.81), channel_id=1, source_target_pairs={{0,1},{1,0},{2,3},{3,2},{4,5},{5,4},{6,7},{7,6},{8,9},{9,8},{10,11... | collective-permute-start | bytes 3145736 | tf_op jit(solution)/shard_map/ppermute | solution.py:111
  1492.2 66.0 %collective-permute-start.24 = (f32[512,512]{1,0:T(8,128)S(1)}, f32[512,512]{1,0:T(8,128)S(1)}, u32[]{:S(2)}, u32[]{:S(2)}) collective-permute-start(f32[512,512]{1,0:T(8,128)S(1)} %get-tuple-element.82), channel_id=1, source_target_pairs={{0,2},{1,3},{2,0},{3,1},{4,6},{5,7},{6,4},{7,5},{8,10},{9,11},{10,... | collective-permute-start | bytes 3145736 | tf_op jit(solution)/shard_map/ppermute | solution.py:111
  1544.0 35.8 %collective-permute-start.25 = (f32[512,512]{1,0:T(8,128)S(1)}, f32[512,512]{1,0:T(8,128)S(1)}, u32[]{:S(2)}, u32[]{:S(2)}) collective-permute-start(f32[512,512]{1,0:T(8,128)S(1)} %get-tuple-element.83), channel_id=1, source_target_pairs={{0,3},{1,2},{2,1},{3,0},{4,7},{5,6},{6,5},{7,4},{8,11},{9,10},{10,... | collective-permute-start | bytes 3145736 | tf_op jit(solution)/shard_map/ppermute | solution.py:111
  1545.7 34.2 %collective-permute-start.26 = (f32[512,512]{1,0:T(8,128)S(1)}, f32[512,512]{1,0:T(8,128)S(1)}, u32[]{:S(2)}, u32[]{:S(2)}) collective-permute-start(f32[512,512]{1,0:T(8,128)S(1)} %get-tuple-element.84), channel_id=1, source_target_pairs={{0,4},{1,5},{2,6},{3,7},{4,0},{5,1},{6,2},{7,3},{8,12},{9,13},{10,... | collective-permute-start | bytes 3145736 | tf_op jit(solution)/shard_map/ppermute | solution.py:111
  1547.2 89.6 %collective-permute-start.27 = (f32[512,512]{1,0:T(8,128)S(1)}, f32[512,512]{1,0:T(8,128)S(1)}, u32[]{:S(2)}, u32[]{:S(2)}) collective-permute-start(f32[512,512]{1,0:T(8,128)S(1)} %get-tuple-element.85), channel_id=1, source_target_pairs={{0,5},{1,4},{2,7},{3,6},{4,1},{5,0},{6,3},{7,2},{8,13},{9,12},{10,... | collective-permute-start | bytes 3145736 | tf_op jit(solution)/shard_map/ppermute | solution.py:111
  1547.3 89.5 %collective-permute-start.28 = (f32[512,512]{1,0:T(8,128)S(1)}, f32[512,512]{1,0:T(8,128)S(1)}, u32[]{:S(2)}, u32[]{:S(2)}) collective-permute-start(f32[512,512]{1,0:T(8,128)S(1)} %get-tuple-element.86), channel_id=1, source_target_pairs={{0,6},{1,7},{2,4},{3,5},{4,2},{5,3},{6,0},{7,1},{8,14},{9,15},{10,... | collective-permute-start | bytes 3145736 | tf_op jit(solution)/shard_map/ppermute | solution.py:111
  1558.3 78.6 %collective-permute-start.29 = (f32[512,512]{1,0:T(8,128)S(1)}, f32[512,512]{1,0:T(8,128)S(1)}, u32[]{:S(2)}, u32[]{:S(2)}) collective-permute-start(f32[512,512]{1,0:T(8,128)S(1)} %get-tuple-element.87), channel_id=1, source_target_pairs={{0,7},{1,6},{2,5},{3,4},{4,3},{5,2},{6,1},{7,0},{8,15},{9,14},{10,... | collective-permute-start | bytes 3145736 | tf_op jit(solution)/shard_map/ppermute | solution.py:111
  (54 other events, 2940.2 us)
Sparse Core Ops, SparseCore 0:
  12.1 246.5 all-gather.6
  261.0 391.3 all-gather.4

commit v4 on v3

--- a/solution.py
+++ b/solution.py
@@ -7,7 +7,7 @@
 NORM_EPS = 1e-6
 MTP_LAMBDA = 0.3
 UNIT = 256
-CHUNKS = (2, 2, 2, 2)
+CHUNKS = (2, 3, 2, 1)
 
 
 def solution(mesh):
@@ -63,12 +63,13 @@
         own_row_w = lax.dynamic_index_in_dim(all_row_w, dp_rank, 0, keepdims=False).reshape(2 * rows)
         probs = jnp.exp(logits - own_lse[:, None])
         grad_z = (own_row_w[:, None] * jnp.where(is_target, probs - 1.0, probs)).astype(jnp.bfloat16)
-        grad_u, gain_parts = [], []
-        for which in range(2):
-            part = lax.dot_general(grad_z[which * rows:(which + 1) * rows], w_out, (((1,), (1,)), ((), ())), preferred_element_type=jnp.float32).astype(jnp.bfloat16).astype(jnp.float32)
-            h, part = lax.optimization_barrier(((h_main, h_mtp)[which], part))
-            gain_parts.append(jnp.sum(part * normalise(h)[0], axis=0))
-            grad_u.append((part, lax.ppermute(part, 'tp', [(i, n_tp - 1 - i) for i in range(n_tp)])))
+        pieces = ((0, 0, rows), (1, 0, rows))
+        grad_u, gain_parts = [], [0.0, 0.0]
+        for which, row, count in pieces:
+            part = lax.dot_general(grad_z[which * rows + row:which * rows + row + count], w_out, (((1,), (1,)), ((), ())), preferred_element_type=jnp.float32).astype(jnp.bfloat16).astype(jnp.float32)
+            h, part = lax.optimization_barrier(((h_main, h_mtp)[which].reshape(rows, d_model)[row:row + count], part))
+            gain_parts[which] += jnp.sum(part * normalise(h)[0], axis=0)
+            grad_u.append((part, lax.ppermute(part, 'tp', [(j, n_tp - 1 - j) for j in range(n_tp)])))
         grad_gain = jnp.stack(gain_parts)
         for axis, size in (('dp', n_dp), ('tp', n_tp)):
             bit = 1
@@ -89,36 +90,44 @@
         def token_order(a):
             return a.reshape(n_dp, n_tp, half).transpose(1, 0, 2).reshape(n_dp * rows)
 
-        def slice_grad(which, u_all, cols, start):
-            z = jnp.dot(u_all, cols, preferred_element_type=jnp.float32)
+        def rows_of(which, other):
+            n, other = lax.optimization_barrier((gathered[which], other))
+            return (n * gains[which]).astype(jnp.bfloat16), other
+
+        def slice_dz(which, cols, start):
+            z = jnp.dot(*rows_of(which, cols), preferred_element_type=jnp.float32)
             hit = (jnp.arange(cols.shape[1], dtype=jnp.int32)[None, :] + start) == token_order(all_labels[:, which])[:, None]
             p = jnp.exp(z - token_order(all_lse[:, which])[:, None])
-            e = (token_order(all_row_w[:, which])[:, None] * jnp.where(hit, p - 1.0, p)).astype(jnp.bfloat16)
-            return lax.dot_general(u_all, e, (((0,), (0,)), ((), ())), preferred_element_type=jnp.float32)
+            return (token_order(all_row_w[:, which])[:, None] * jnp.where(hit, p - 1.0, p)).astype(jnp.bfloat16)
 
-        u_all = [(n * g).astype(jnp.bfloat16) for n, g in zip(gathered, gains)]
+        def slice_grad(which, e):
+            return lax.dot_general(*rows_of(which, e), (((0,), (0,)), ((), ())), preferred_element_type=jnp.float32)
+
         d_loc = d_model // n_dp
         grad_w = jnp.zeros((d_loc, shard_vocab), jnp.float32)
-        grad_main = slice_grad(0, u_all[0], w_slice, slice_start)
+        grad_main = slice_grad(0, slice_dz(0, w_slice, slice_start))
+        dz_mtp, split = [], sum(CHUNKS[:2]) * UNIT
+        for lo, hi in ((0, split), (split, width)):
+            dz_mtp.append(slice_dz(1, w_slice[:, lo:hi], slice_start + lo))
         for q, chunk in enumerate(CHUNKS):
             done = sum(CHUNKS[:q])
             lo, cw = done * UNIT, chunk * UNIT
-            cols = w_slice[:, lo:lo + cw]
-            part = grad_main[:, lo:lo + cw] + slice_grad(1, u_all[1], cols, slice_start + lo)
+            dz = (dz_mtp[0][:, lo:] if lo < split else dz_mtp[1][:, lo - split:])[:, :cw]
+            part = grad_main[:, lo:lo + cw] + slice_grad(1, dz)
             sends = lax.optimization_barrier([lax.dynamic_slice(part, ((dp_rank ^ k) * d_loc, 0), (d_loc, cw)) for k in range(n_dp)])
             for k, block in enumerate(sends):
                 if k:
                     block = lax.ppermute(block, 'dp', [(i, i ^ k) for i in range(n_dp)])
                 grad_w = lax.dynamic_update_slice(grad_w, block, (0, (first_unit(dp_rank ^ k) + done) * UNIT))
 
-        grads_h = []
-        for which, h in enumerate((h_main, h_mtp)):
-            h, part, other = lax.optimization_barrier((h, *grad_u[which]))
+        grads_h = [[], []]
+        for (which, row, count), (part, other) in zip(pieces, grad_u):
+            h, part, other = lax.optimization_barrier(((h_main, h_mtp)[which].reshape(rows, d_model)[row:row + count], part, other))
             n, inv = normalise(h)
-            du = part + other
-            grad_normed = du * gains[which]
+            grad_normed = (part + other) * gains[which]
             grad_x = inv * (grad_normed - n * jnp.mean(grad_normed * n, axis=-1, keepdims=True))
-            grads_h.append(grad_x.astype(jnp.bfloat16).reshape(batch_loc, seq_len, d_model))
+            grads_h[which].append(grad_x.astype(jnp.bfloat16))
+        grads_h = [jnp.concatenate(g).reshape(batch_loc, seq_len, d_model) for g in grads_h]
         return loss_total, grads_h[0], grads_h[1], grad_w, grad_gain[0], grad_gain[1]
 
 

time: 1660 us -> 1660 us (level)
  local copies, waits for them, and re-layouts: 68.5 us -> 99.4 us
  other arithmetic: 160 us -> 131 us
    ppermute x4, waiting for transfers between devices: 406 us -> 370 us  [layer_step(): lax.ppermute(grad_gain, axis, [(i, i ^ bit) for i in range(size)])]
    convert_element_type x1 -> x0, other arithmetic: 32.7 us -> none  [layer_step(): u_all = [(n * g).astype(jnp.bfloat16) for n, g in zip(gathered, gains)]]
    ppermute x28, waiting for transfers between devices: 253 us -> 279 us  [layer_step(): block = lax.ppermute(block, 'dp', [(i, i ^ k) for i in range(n_dp)])]
    slice x2 -> x9, local copies, waits for them, and re-layouts: 0.24 us -> 24.6 us  [the longest x2 14.6 us: layer_step(): dz_mtp.append(slice_dz(1, w_slice[:, lo:hi], slice_start + lo))]
    dot_general x12 -> x10, matrix products: 551 us -> 551 us  [the longest x5 210 us: slice_grad(): lax.dot_general(*rows_of(which, e), (((0,), (0,)), ((), ())), preferred_e...]
  transfers between devices with their start and end apart: 36 -> 36, of which waited for: 14 -> 13; matrix products, arithmetic and copies ran while one was open for 36% -> 43% of each run, Pallas kernels for 0% -> 0%
where the time goes in v4:
time: 1660 us; the launch traced here: 1650 us
  matrix products  699 us (42%)
  waiting for transfers between devices  649 us (39%)
  other arithmetic  131 us (8%)
  local copies, waits for them, and re-layouts  99.4 us (6%)
  starting transfers between devices  40.3 us (2%)
  blocking collectives  18 us (1%)
    ppermute x4, waiting for transfers between devices, layer_step(): lax.ppermute(grad_gain, axis, [(i, i ^ bit) for i in range(size)])  370 us
    ppermute x28, waiting for transfers between devices, layer_step(): block = lax.ppermute(block, 'dp', [(i, i ^ k) for i in range(n_dp)])  279 us
    dot_general x5, matrix products, slice_grad(): lax.dot_general(*rows_of(which, e), (((0,), (0,)), ((), ())), preferred_e...  210 us
    dot_general x3, matrix products, slice_dz(): z = jnp.dot(*rows_of(which, cols), preferred_element_type=jnp.float32)  174 us
    dot_general x2, matrix products, layer_step(): lax.dot_general(grad_z[which * rows + row:which * rows + row + count], w_...  166 us
    dot_general x1, matrix products, layer_step(): logits = jnp.dot(u_rows, w_out, preferred_element_type=jnp.float32)  148 us
    convert_element_type x1, other arithmetic, layer_step(): (own_row_w[:, None] * jnp.where(is_target, probs - 1.0, probs)).astype(jn...  34.9 us
  transfers between devices with their start and end apart: 36, of which 13 were waited for; matrix products, arithmetic and copies ran while one was open for 43% of the time, Pallas kernels for 0%

profile of v4, /device:TPU:0, one launch (start us, length us, event | category | flops | bytes accessed | tf_op | source)
XLA Modules:
  0.0 1652.7 jit_solution(16130469605592329400)
XLA Ops:
  31.1 148.2 %fusion.86 = (f32[1024]{0:T(1024)S(1)}, f32[1024,16128]{1,0:T(8,128)}) fusion(bf16[4096,16128]{1,0:T(8,128)(2,1)} %param.18, bf16[512,4096]{1,0:T(8,128)(2,1)S(1)} %fusion.45, bf16[512,4096]{1,0:T(8,128)(2,1)S(1)} %fusion.42), kind=kOutput, calls=%fused_computation.217 | convolution fusion | flops 135324762112 | bytes 206573568 | tf_op jit(solution)/shard_map/dot_general | solution.py:44
  179.4 24.7 %select_reduce_fusion = (f32[1024]{0:T(1024)S(1)}, f32[1024]{0:T(1024)S(1)}) fusion(f32[1024,16128]{1,0:T(8,128)} %get-tuple-element.170, s32[1024]{0:T(1024)S(1)} %copy-done.27, f32[1024]{0:T(1024)S(1)} %get-tuple-element.169), kind=kLoop, calls=%fused_computation.11 | loop fusion | flops 82573312 | bytes 66076672 | tf_op jit(solution)/shard_map/reduce_sum | solution.py:48
  204.1 18.0 %all-gather.1 = f32[16,5,1024]{2,1,0:T(8,128)S(1)} all-gather(f32[1,5,1024]{2,1,0:T(8,128)S(1)} %bitcast.137), channel_id=2, replica_groups=mesh['tp'=2,'dp'=8] {'tp','dp'}, dimensions={0}, use_global_device_ids=true | all-gather | bytes 348160 | tf_op jit(solution)/shard_map/all_gather | solution.py:51
  224.0 34.9 %fusion.1 = bf16[1024,16128]{1,0:T(8,128)(2,1)} fusion(f32[1024,16128]{1,0:T(8,128)} %get-tuple-element.170, f32[1024]{0:T(1024)S(1)} %bitcast.145, f32[1024]{0:T(1024)S(1)} %bitcast.144, s32[1024]{0:T(1024)S(1)} %copy-done.27), kind=kLoop, calls=%fused_computation.10 | loop fusion | flops 99090432 | bytes 99102720 | tf_op jit(solution)/shard_map/convert_element_type | solution.py:65
  258.9 82.8 %fusion.67 = f32[512,4096]{1,0:T(8,128)} fusion(bf16[4096,16128]{1,0:T(8,128)(2,1)} %param.18, bf16[1024,16128]{1,0:T(8,128)(2,1)} %fusion.1), kind=kOutput, calls=%fused_computation.93 | convolution fusion | flops 67649929216 | bytes 157024256 | tf_op jit(solution)/shard_map/dot_general | solution.py:69
  342.7 83.5 %fusion.61 = f32[512,4096]{1,0:T(8,128)} fusion(bf16[4096,16128]{1,0:T(8,128)(2,1)} %param.18, bf16[1024,16128]{1,0:T(8,128)(2,1)} %fusion.1), kind=kOutput, calls=%fused_computation.91 | convolution fusion | flops 67649929216 | bytes 157024256 | tf_op jit(solution)/shard_map/dot_general | solution.py:69
  448.3 14.2 constant_dynamic-slice_fusion.34
  462.5 8.8 constant_dynamic-slice_fusion.1
  486.8 365.2 %collective-permute-done.33 = f32[2,4096]{1,0:T(2,128)S(1)} collective-permute-done((f32[2,4096]{1,0:T(2,128)S(1)}, f32[2,4096]{1,0:T(2,128)S(1)}, u32[]{:S(2)}, u32[]{:S(2)}) %collective-permute-start.33) | collective-permute-done | bytes 32800 | tf_op jit(solution)/shard_map/ppermute | solution.py:77
  855.8 8.0 fusion.32
  864.8 7.3 fusion.36
  873.6 6.9 fusion.74
  887.2 53.0 %fusion.21 = bf16[4096,1280]{1,0:T(8,128)(2,1)S(1)} fusion(bf16[4096,1280]{1,0:T(8,128)(2,1)} %constant_dynamic-slice_fusion.1, f32[4096,4096]{1,0:T(8,128)} %all-gather.7.cloned.1.call-done, f32[4096]{0:T(1024)S(1)} %copy-done.18, f32[4096]{0:T(1024)S(1)} %bitcast.151, s32[1280]{0:T(1024)S(1)} %iota_add_fusion, f32[4096]{0:T(1024)S(1)} %bitcast.149, ...), kind=kOutput, calls=%fused_computation.35 | convolution fusion | flops 43014684672 | bytes 88151040 | tf_op jit(solution)/shard_map/dot_general | solution.py:98
  945.5 84.4 %fusion.3 = bf16[4096,2048]{1,0:T(8,128)(2,1)} fusion(bf16[4096,2048]{1,0:T(8,128)(2,1)} %constant_dynamic-slice_fusion.34, f32[4096,4096]{1,0:T(8,128)} %all-gather.5.cloned.1.call-done, f32[4096]{0:T(1024)S(1)} %copy-done.26, f32[4096]{0:T(1024)S(1)} %bitcast.156, s32[2048]{0:T(1024)S(1)} %copy-done.39, f32[4096]{0:T(1024)S(1)} %bitcast.155, ...), kind=kOutput, calls=%fused_computation.16 | convolution fusion | flops 68803362816 | bytes 100737024 | tf_op jit(solution)/shard_map/dot_general | solution.py:98
  1029.9 82.6 %fusion.5 = f32[4096,2048]{1,0:T(8,128)} fusion(bf16[4096,2048]{1,0:T(8,128)(2,1)} %fusion.3, f32[4096,4096]{1,0:T(8,128)} %all-gather.5.cloned.1.call-done, f32[4096]{0:T(1024)S(1)} %copy-done.26), kind=kOutput, calls=%fused_computation.18 | convolution fusion | flops 68753031168 | bytes 117456896 | tf_op jit(solution)/shard_map/dot_general | solution.py:104
  1112.5 31.8 %slice_add_fusion.2 = f32[4096,512]{1,0:T(8,128)} fusion(f32[4096,2048]{1,0:T(8,128)} %fusion.5, bf16[4096,512]{1,0:T(8,128)(2,1)} %slice.118, f32[4096,4096]{1,0:T(8,128)} %all-gather.7.cloned.1.call-done, f32[4096]{0:T(1024)S(1)} %copy-done.19), kind=kOutput, calls=%fused_computation.83 | convolution fusion | flops 17215520768 | bytes 88096768 | tf_op jit(solution)/shard_map/dot_general | solution.py:104
  1150.9 36.7 %fusion.27 = bf16[4096,768]{1,0:T(8,128)(2,1)} fusion(bf16[4096,768]{1,0:T(8,128)(2,1)} %constant_dynamic-slice_fusion, f32[4096,4096]{1,0:T(8,128)} %all-gather.7.cloned.1.call-done, f32[4096]{0:T(1024)S(1)} %copy-done.19, f32[4096]{0:T(1024)S(1)} %bitcast.152, s32[768]{0:T(1024)S(1)} %copy-done.42, f32[4096]{0:T(1024)S(1)} %bitcast.150, ...), kind=kOutput, calls=%fused_computation.42 | convolution fusion | flops 25822232576 | bytes 79760384 | tf_op jit(solution)/shard_map/dot_general | solution.py:98
  1187.6 39.3 %slice_add_fusion = f32[4096,768]{1,0:T(8,128)} fusion(f32[4096,2048]{1,0:T(8,128)} %fusion.5, bf16[4096,768]{1,0:T(8,128)(2,1)} %slice.120, f32[4096,4096]{1,0:T(8,128)} %all-gather.7.cloned.1.call-done, f32[4096]{0:T(1024)S(1)} %copy-done.19), kind=kOutput, calls=%fused_computation.43 | convolution fusion | flops 25806503936 | bytes 98582528 | tf_op jit(solution)/shard_map/dot_general | solution.py:104
  1237.2 31.7 %slice_add_fusion.1 = f32[4096,512]{1,0:T(8,128)} fusion(f32[4096,2048]{1,0:T(8,128)} %fusion.5, bf16[4096,512]{1,0:T(8,128)(2,1)} %slice.122, f32[4096,4096]{1,0:T(8,128)} %all-gather.7.cloned.1.call-done, f32[4096]{0:T(1024)S(1)} %copy-done.19), kind=kOutput, calls=%fused_computation.82 | convolution fusion | flops 17215520768 | bytes 88096768 | tf_op jit(solution)/shard_map/dot_general | solution.py:104
  1268.9 6.9 constant_dynamic-slice_fusion.10
  1275.8 9.0 constant_dynamic-slice_fusion.18
  1286.9 38.3 %collective-permute-done.6 = f32[512,512]{1,0:T(8,128)} collective-permute-done((f32[512,512]{1,0:T(8,128)}, f32[512,512]{1,0:T(8,128)}, u32[]{:S(2)}, u32[]{:S(2)}) %collective-permute-start.6) | collective-permute-done | bytes 1048608 | tf_op jit(solution)/shard_map/ppermute | solution.py:120
  1327.8 24.9 %fusion.70 = f32[4096,256]{1,0:T(8,128)S(1)} fusion(bf16[4096,256]{1,0:T(8,128)(2,1)S(1)} %slice-done.6, f32[4096,4096]{1,0:T(8,128)} %all-gather.7.cloned.1.call-done, f32[4096]{0:T(1024)S(1)} %copy-done.19, f32[4096,2048]{1,0:T(8,128)} %fusion.5), kind=kOutput, calls=%fused_computation.94 | convolution fusion | flops 8624537600 | bytes 77611008 | tf_op jit(solution)/shard_map/dot_general | solution.py:104
  1358.7 22.6 %collective-permute-done.17 = f32[512,512]{1,0:T(8,128)} collective-permute-done((f32[512,512]{1,0:T(8,128)}, f32[512,512]{1,0:T(8,128)}, u32[]{:S(2)}, u32[]{:S(2)}) %collective-permute-start.17) | collective-permute-done | bytes 1048608 | tf_op jit(solution)/shard_map/ppermute | solution.py:120
  1396.3 17.7 %collective-permute-done.11 = f32[512,768]{1,0:T(8,128)S(1)} collective-permute-done((f32[512,768]{1,0:T(8,128)}, f32[512,768]{1,0:T(8,128)S(1)}, u32[]{:S(2)}, u32[]{:S(2)}) %collective-permute-start.11) | collective-permute-done | bytes 1572896 | tf_op jit(solution)/shard_map/ppermute | solution.py:120
  1417.8 77.2 %collective-permute-done.13 = f32[512,768]{1,0:T(8,128)S(1)} collective-permute-done((f32[512,768]{1,0:T(8,128)S(1)}, f32[512,768]{1,0:T(8,128)S(1)}, u32[]{:S(2)}, u32[]{:S(2)}) %collective-permute-start.13) | collective-permute-done | bytes 1572896 | tf_op jit(solution)/shard_map/ppermute | solution.py:120
  1505.0 58.1 %collective-permute-done.19 = f32[512,512]{1,0:T(8,128)S(1)} collective-permute-done((f32[512,512]{1,0:T(8,128)}, f32[512,512]{1,0:T(8,128)S(1)}, u32[]{:S(2)}, u32[]{:S(2)}) %collective-permute-start.19) | collective-permute-done | bytes 1048608 | tf_op jit(solution)/shard_map/ppermute | solution.py:120
  1564.5 20.4 %collective-permute-done.20 = f32[512,512]{1,0:T(8,128)S(1)} collective-permute-done((f32[512,512]{1,0:T(8,128)}, f32[512,512]{1,0:T(8,128)S(1)}, u32[]{:S(2)}, u32[]{:S(2)}) %collective-permute-start.20) | collective-permute-done | bytes 1048608 | tf_op jit(solution)/shard_map/ppermute | solution.py:120
  1591.2 7.8 collective-permute-done.25
  1599.1 24.8 %collective-permute-done.26 = f32[512,256]{1,0:T(8,128)S(1)} collective-permute-done((f32[512,256]{1,0:T(8,128)}, f32[512,256]{1,0:T(8,128)S(1)}, u32[]{:S(2)}, u32[]{:S(2)}) %collective-permute-start.26) | collective-permute-done | bytes 524320 | tf_op jit(solution)/shard_map/ppermute | solution.py:120
  1623.9 10.0 collective-permute-done.27
  1634.1 11.5 copy-done.4
  (268 shorter events, 146.1 us)
Async XLA Ops:
  7.2 880.0 %all-gather.7.cloned.1.call-start = ((), (), s32[]{:S(2)}) async-start(), calls=%async_computation.1 | async-start | bytes 71303168 | tf_op jit(solution)/shard_map/all_gather | solution.py:34
  12.9 932.6 %all-gather.5.cloned.1.call-start = ((), (), s32[]{:S(2)}) async-start(), calls=%async_computation | async-start | bytes 71303168 | tf_op jit(solution)/shard_map/all_gather | solution.py:34
  341.7 511.0 %collective-permute-start.1 = (f32[512,4096]{1,0:T(8,128)}, f32[512,4096]{1,0:T(8,128)}, u32[]{:S(2)}, u32[]{:S(2)}) collective-permute-start(f32[512,4096]{1,0:T(8,128)} %fusion.67), channel_id=1, source_target_pairs={{0,8},{8,0},{1,9},{9,1},{2,10},{10,2},{3,11},{11,3},{4,12},{12,4},... | collective-permute-start | bytes 25165832 | tf_op jit(solution)/shard_map/ppermute | solution.py:72
  426.2 426.5 %collective-permute-start = (f32[512,4096]{1,0:T(8,128)}, f32[512,4096]{1,0:T(8,128)}, u32[]{:S(2)}, u32[]{:S(2)}) collective-permute-start(f32[512,4096]{1,0:T(8,128)} %fusion.61), channel_id=1, source_target_pairs={{0,8},{8,0},{1,9},{9,1},{2,10},{10,2},{3,11},{11,3},{4,12},{12,4},... | collective-permute-start | bytes 25165832 | tf_op jit(solution)/shard_map/ppermute | solution.py:72
  441.5 29.9 %collective-permute-start.30 = (f32[2,4096]{1,0:T(2,128)S(1)}, f32[2,4096]{1,0:T(2,128)S(1)}, u32[]{:S(2)}, u32[]{:S(2)}) collective-permute-start(f32[2,4096]{1,0:T(2,128)S(1)} %pad_maximum_fusion), channel_id=1, source_target_pairs={{0,1},{1,0},{2,3},{3,2},{4,5},{5,4},{6,7},{7,6},{8,9},{9,8},{10,11... | collective-permute-start | bytes 98312 | tf_op jit(solution)/shard_map/ppermute | solution.py:77
  481.2 370.8 %collective-permute-start.33 = (f32[2,4096]{1,0:T(2,128)S(1)}, f32[2,4096]{1,0:T(2,128)S(1)}, u32[]{:S(2)}, u32[]{:S(2)}) collective-permute-start(f32[2,4096]{1,0:T(2,128)S(1)} %add.457), channel_id=1, source_target_pairs={{0,8},{8,0},{1,9},{9,1},{2,10},{10,2},{3,11},{11,3},{4,12},{12,4},... | collective-permute-start | bytes 98312 | tf_op jit(solution)/shard_map/ppermute | solution.py:77
  1150.8 84.0 %collective-permute-start.2 = (f32[512,512]{1,0:T(8,128)S(1)}, f32[512,512]{1,0:T(8,128)S(1)}, u32[]{:S(2)}, u32[]{:S(2)}) collective-permute-start(f32[512,512]{1,0:T(8,128)S(1)} %get-tuple-element.81), channel_id=1, source_target_pairs={{0,1},{1,0},{2,3},{3,2},{4,5},{5,4},{6,7},{7,6},{8,9},{9,8},{10,11... | collective-permute-start | bytes 3145736 | tf_op jit(solution)/shard_map/ppermute | solution.py:120
  1231.3 53.5 %collective-permute-start.3 = (f32[512,512]{1,0:T(8,128)}, f32[512,512]{1,0:T(8,128)}, u32[]{:S(2)}, u32[]{:S(2)}) collective-permute-start(f32[512,512]{1,0:T(8,128)} %get-tuple-element.82), channel_id=1, source_target_pairs={{0,2},{1,3},{2,0},{3,1},{4,6},{5,7},{6,4},{7,5},{8,10},{9,11},{10,... | collective-permute-start | bytes 3145736 | tf_op jit(solution)/shard_map/ppermute | solution.py:120
  1232.8 52.5 %collective-permute-start.4 = (f32[512,512]{1,0:T(8,128)}, f32[512,512]{1,0:T(8,128)}, u32[]{:S(2)}, u32[]{:S(2)}) collective-permute-start(f32[512,512]{1,0:T(8,128)} %get-tuple-element.83), channel_id=1, source_target_pairs={{0,3},{1,2},{2,1},{3,0},{4,7},{5,6},{6,5},{7,4},{8,11},{9,10},{10,... | collective-permute-start | bytes 3145736 | tf_op jit(solution)/shard_map/ppermute | solution.py:120
  1233.1 52.3 %collective-permute-start.5 = (f32[512,512]{1,0:T(8,128)}, f32[512,512]{1,0:T(8,128)}, u32[]{:S(2)}, u32[]{:S(2)}) collective-permute-start(f32[512,512]{1,0:T(8,128)} %get-tuple-element.84), channel_id=1, source_target_pairs={{0,4},{1,5},{2,6},{3,7},{4,0},{5,1},{6,2},{7,3},{8,12},{9,13},{10,... | collective-permute-start | bytes 3145736 | tf_op jit(solution)/shard_map/ppermute | solution.py:120
  1234.6 90.6 %collective-permute-start.6 = (f32[512,512]{1,0:T(8,128)}, f32[512,512]{1,0:T(8,128)}, u32[]{:S(2)}, u32[]{:S(2)}) collective-permute-start(f32[512,512]{1,0:T(8,128)} %get-tuple-element.85), channel_id=1, source_target_pairs={{0,5},{1,4},{2,7},{3,6},{4,1},{5,0},{6,3},{7,2},{8,13},{9,12},{10,... | collective-permute-start | bytes 3145736 | tf_op jit(solution)/shard_map/ppermute | solution.py:120
  1234.8 91.6 %collective-permute-start.7 = (f32[512,512]{1,0:T(8,128)}, f32[512,512]{1,0:T(8,128)}, u32[]{:S(2)}, u32[]{:S(2)}) collective-permute-start(f32[512,512]{1,0:T(8,128)} %get-tuple-element.86), channel_id=1, source_target_pairs={{0,6},{1,7},{2,4},{3,5},{4,2},{5,3},{6,0},{7,1},{8,14},{9,15},{10,... | collective-permute-start | bytes 3145736 | tf_op jit(solution)/shard_map/ppermute | solution.py:120
  1284.8 68.0 %collective-permute-start.8 = (f32[512,512]{1,0:T(8,128)}, f32[512,512]{1,0:T(8,128)}, u32[]{:S(2)}, u32[]{:S(2)}) collective-permute-start(f32[512,512]{1,0:T(8,128)} %get-tuple-element.87), channel_id=1, source_target_pairs={{0,7},{1,6},{2,5},{3,4},{4,3},{5,2},{6,1},{7,0},{8,15},{9,14},{10,... | collective-permute-start | bytes 3145736 | tf_op jit(solution)/shard_map/ppermute | solution.py:120
  1285.2 97.6 %collective-permute-start.9 = (f32[512,768]{1,0:T(8,128)}, f32[512,768]{1,0:T(8,128)}, u32[]{:S(2)}, u32[]{:S(2)}) collective-permute-start(f32[512,768]{1,0:T(8,128)} %get-tuple-element.91), channel_id=1, source_target_pairs={{0,1},{1,0},{2,3},{3,2},{4,5},{5,4},{6,7},{7,6},{8,9},{9,8},{10,11... | collective-permute-start | bytes 4718600 | tf_op jit(solution)/shard_map/ppermute | solution.py:120
  1285.5 100.9 %collective-permute-start.10 = (f32[512,768]{1,0:T(8,128)}, f32[512,768]{1,0:T(8,128)}, u32[]{:S(2)}, u32[]{:S(2)}) collective-permute-start(f32[512,768]{1,0:T(8,128)} %get-tuple-element.92), channel_id=1, source_target_pairs={{0,2},{1,3},{2,0},{3,1},{4,6},{5,7},{6,4},{7,5},{8,10},{9,11},{10,... | collective-permute-start | bytes 4718600 | tf_op jit(solution)/shard_map/ppermute | solution.py:120
  1325.2 31.8 %collective-permute-start.16 = (f32[512,512]{1,0:T(8,128)}, f32[512,512]{1,0:T(8,128)}, u32[]{:S(2)}, u32[]{:S(2)}) collective-permute-start(f32[512,512]{1,0:T(8,128)} %get-tuple-element.103), channel_id=1, source_target_pairs={{0,1},{1,0},{2,3},{3,2},{4,5},{5,4},{6,7},{7,6},{8,9},{9,8},{10,11... | collective-permute-start | bytes 3145736 | tf_op jit(solution)/shard_map/ppermute | solution.py:120
  1326.4 54.9 %collective-permute-start.17 = (f32[512,512]{1,0:T(8,128)}, f32[512,512]{1,0:T(8,128)}, u32[]{:S(2)}, u32[]{:S(2)}) collective-permute-start(f32[512,512]{1,0:T(8,128)} %get-tuple-element.104), channel_id=1, source_target_pairs={{0,2},{1,3},{2,0},{3,1},{4,6},{5,7},{6,4},{7,5},{8,10},{9,11},{10,... | collective-permute-start | bytes 3145736 | tf_op jit(solution)/shard_map/ppermute | solution.py:120
  1352.8 61.2 %collective-permute-start.11 = (f32[512,768]{1,0:T(8,128)}, f32[512,768]{1,0:T(8,128)S(1)}, u32[]{:S(2)}, u32[]{:S(2)}) collective-permute-start(f32[512,768]{1,0:T(8,128)} %get-tuple-element.93), channel_id=1, source_target_pairs={{0,3},{1,2},{2,1},{3,0},{4,7},{5,6},{6,5},{7,4},{8,11},{9,10},{10,... | collective-permute-start | bytes 4718600 | tf_op jit(solution)/shard_map/ppermute | solution.py:120
  1357.1 59.1 %collective-permute-start.12 = (f32[512,768]{1,0:T(8,128)}, f32[512,768]{1,0:T(8,128)S(1)}, u32[]{:S(2)}, u32[]{:S(2)}) collective-permute-start(f32[512,768]{1,0:T(8,128)} %get-tuple-element.94), channel_id=1, source_target_pairs={{0,4},{1,5},{2,6},{3,7},{4,0},{5,1},{6,2},{7,3},{8,12},{9,13},{10,... | collective-permute-start | bytes 4718600 | tf_op jit(solution)/shard_map/ppermute | solution.py:120
  1381.3 113.8 %collective-permute-start.13 = (f32[512,768]{1,0:T(8,128)S(1)}, f32[512,768]{1,0:T(8,128)S(1)}, u32[]{:S(2)}, u32[]{:S(2)}) collective-permute-start(f32[512,768]{1,0:T(8,128)S(1)} %copy-done.9), channel_id=1, source_target_pairs={{0,5},{1,4},{2,7},{3,6},{4,1},{5,0},{6,3},{7,2},{8,13},{9,12},{10,... | collective-permute-start | bytes 4718600 | tf_op jit(solution)/shard_map/ppermute | solution.py:120
  1382.8 114.2 %collective-permute-start.14 = (f32[512,768]{1,0:T(8,128)S(1)}, f32[512,768]{1,0:T(8,128)S(1)}, u32[]{:S(2)}, u32[]{:S(2)}) collective-permute-start(f32[512,768]{1,0:T(8,128)S(1)} %copy-done.8), channel_id=1, source_target_pairs={{0,6},{1,7},{2,4},{3,5},{4,2},{5,3},{6,0},{7,1},{8,14},{9,15},{10,... | collective-permute-start | bytes 4718600 | tf_op jit(solution)/shard_map/ppermute | solution.py:120
  1386.4 112.1 %collective-permute-start.15 = (f32[512,768]{1,0:T(8,128)S(1)}, f32[512,768]{1,0:T(8,128)S(1)}, u32[]{:S(2)}, u32[]{:S(2)}) collective-permute-start(f32[512,768]{1,0:T(8,128)S(1)} %copy-done.7), channel_id=1, source_target_pairs={{0,7},{1,6},{2,5},{3,4},{4,3},{5,2},{6,1},{7,0},{8,15},{9,14},{10,... | collective-permute-start | bytes 4718600 | tf_op jit(solution)/shard_map/ppermute | solution.py:120
  1414.0 89.9 %collective-permute-start.18 = (f32[512,512]{1,0:T(8,128)}, f32[512,512]{1,0:T(8,128)S(1)}, u32[]{:S(2)}, u32[]{:S(2)}) collective-permute-start(f32[512,512]{1,0:T(8,128)} %get-tuple-element.105), channel_id=1, source_target_pairs={{0,3},{1,2},{2,1},{3,0},{4,7},{5,6},{6,5},{7,4},{8,11},{9,10},{10,... | collective-permute-start | bytes 3145736 | tf_op jit(solution)/shard_map/ppermute | solution.py:120
  1416.2 146.9 %collective-permute-start.19 = (f32[512,512]{1,0:T(8,128)}, f32[512,512]{1,0:T(8,128)S(1)}, u32[]{:S(2)}, u32[]{:S(2)}) collective-permute-start(f32[512,512]{1,0:T(8,128)} %get-tuple-element.106), channel_id=1, source_target_pairs={{0,4},{1,5},{2,6},{3,7},{4,0},{5,1},{6,2},{7,3},{8,12},{9,13},{10,... | collective-permute-start | bytes 3145736 | tf_op jit(solution)/shard_map/ppermute | solution.py:120
  1495.1 89.9 %collective-permute-start.20 = (f32[512,512]{1,0:T(8,128)}, f32[512,512]{1,0:T(8,128)S(1)}, u32[]{:S(2)}, u32[]{:S(2)}) collective-permute-start(f32[512,512]{1,0:T(8,128)} %get-tuple-element.107), channel_id=1, source_target_pairs={{0,5},{1,4},{2,7},{3,6},{4,1},{5,0},{6,3},{7,2},{8,13},{9,12},{10,... | collective-permute-start | bytes 3145736 | tf_op jit(solution)/shard_map/ppermute | solution.py:120
  1497.0 89.3 %collective-permute-start.21 = (f32[512,512]{1,0:T(8,128)}, f32[512,512]{1,0:T(8,128)S(1)}, u32[]{:S(2)}, u32[]{:S(2)}) collective-permute-start(f32[512,512]{1,0:T(8,128)} %get-tuple-element.108), channel_id=1, source_target_pairs={{0,6},{1,7},{2,4},{3,5},{4,2},{5,3},{6,0},{7,1},{8,14},{9,15},{10,... | collective-permute-start | bytes 3145736 | tf_op jit(solution)/shard_map/ppermute | solution.py:120
  1498.5 89.4 %collective-permute-start.22 = (f32[512,512]{1,0:T(8,128)S(1)}, f32[512,512]{1,0:T(8,128)S(1)}, u32[]{:S(2)}, u32[]{:S(2)}) collective-permute-start(f32[512,512]{1,0:T(8,128)S(1)} %copy-done.11), channel_id=1, source_target_pairs={{0,7},{1,6},{2,5},{3,4},{4,3},{5,2},{6,1},{7,0},{8,15},{9,14},{10,... | collective-permute-start | bytes 3145736 | tf_op jit(solution)/shard_map/ppermute | solution.py:120
  1503.9 84.5 %collective-permute-start.23 = (f32[512,256]{1,0:T(8,128)}, f32[512,256]{1,0:T(8,128)S(1)}, u32[]{:S(2)}, u32[]{:S(2)}) collective-permute-start(f32[512,256]{1,0:T(8,128)} %get-tuple-element.113), channel_id=1, source_target_pairs={{0,1},{1,0},{2,3},{3,2},{4,5},{5,4},{6,7},{7,6},{8,9},{9,8},{10,11... | collective-permute-start | bytes 1572872 | tf_op jit(solution)/shard_map/ppermute | solution.py:120
  1586.4 37.5 %collective-permute-start.26 = (f32[512,256]{1,0:T(8,128)}, f32[512,256]{1,0:T(8,128)S(1)}, u32[]{:S(2)}, u32[]{:S(2)}) collective-permute-start(f32[512,256]{1,0:T(8,128)} %get-tuple-element.116), channel_id=1, source_target_pairs={{0,4},{1,5},{2,6},{3,7},{4,0},{5,1},{6,2},{7,3},{8,12},{9,13},{10,... | collective-permute-start | bytes 1572872 | tf_op jit(solution)/shard_map/ppermute | solution.py:120
  1588.0 46.0 %collective-permute-start.27 = (f32[512,256]{1,0:T(8,128)S(1)}, f32[512,256]{1,0:T(8,128)S(1)}, u32[]{:S(2)}, u32[]{:S(2)}) collective-permute-start(f32[512,256]{1,0:T(8,128)S(1)} %copy-done.16), channel_id=1, source_target_pairs={{0,5},{1,4},{2,7},{3,6},{4,1},{5,0},{6,3},{7,2},{8,13},{9,12},{10,... | collective-permute-start | bytes 1572872 | tf_op jit(solution)/shard_map/ppermute | solution.py:120
  1588.4 45.6 %collective-permute-start.28 = (f32[512,256]{1,0:T(8,128)S(1)}, f32[512,256]{1,0:T(8,128)S(1)}, u32[]{:S(2)}, u32[]{:S(2)}) collective-permute-start(f32[512,256]{1,0:T(8,128)S(1)} %copy-done.15), channel_id=1, source_target_pairs={{0,6},{1,7},{2,4},{3,5},{4,2},{5,3},{6,0},{7,1},{8,14},{9,15},{10,... | collective-permute-start | bytes 1572872 | tf_op jit(solution)/shard_map/ppermute | solution.py:120
  1589.8 44.2 %collective-permute-start.29 = (f32[512,256]{1,0:T(8,128)S(1)}, f32[512,256]{1,0:T(8,128)S(1)}, u32[]{:S(2)}, u32[]{:S(2)}) collective-permute-start(f32[512,256]{1,0:T(8,128)S(1)} %copy-done.14), channel_id=1, source_target_pairs={{0,7},{1,6},{2,5},{3,4},{4,3},{5,2},{6,1},{7,0},{8,15},{9,14},{10,... | collective-permute-start | bytes 1572872 | tf_op jit(solution)/shard_map/ppermute | solution.py:120
  (57 other events, 3998.8 us)
Sparse Core Ops, SparseCore 0:
  13.0 246.5 all-gather.6
  261.9 390.4 all-gather.4
